TPU v7x, 32 devices: a whole 2x2x4 slice. The times are simulated.
32 devices in a mesh: win: 8 (over z, x), fsdp: 4 (over y, core).
Axes of the slice: x: 2, y: 2, z: 4, core: 2. Of those that a mesh axis runs over, the one named last changes fastest.
Arguments:
- queries: bfloat16 [8192, 2560], P(('win', 'fsdp')), may hold values from -5 to 5
- keys: bfloat16 [8192, 2560], P(('win', 'fsdp')), may hold values from -5 to 5
- values: bfloat16 [8192, 2560], P(('win', 'fsdp')), may hold values from -6 to 6
- stream: bfloat16 [8192, 5120], P(('win', 'fsdp')), may hold values from -0.59765625 to 0.59765625
- out_weight: bfloat16 [2560, 5120], P('fsdp', 'win'), may hold values from -0.125 to 0.125
- gate: float32 [5120], replicated, may hold values from 0.5 to 2
- head_shift: float32 [5120], replicated, may hold values from -3 to 3
- head_scale: float32 [5120], replicated, may hold values from 0.25 to 1.75
- head_weight: bfloat16 [5120, 64], replicated, may hold values from -0.078125 to 0.078125
- latents: float32 [128, 4096], P('win', 'fsdp'), may hold values from -6 to 6
- step_size: float32 [1], replicated, may hold values from 0.5 to 1
- intersections: int32 [8], replicated, may hold values from 1 to 4
- ramps: int32 [8, 4, 2], replicated, may hold values from 1 to 16
Outputs:
- blended: float32 [128, 4096], P('win', 'fsdp')
All inputs are finite; a program needn't handle non-finite values.
Results may differ from a plain program's by a relative error of at most 0.0065.
Values may be sent and summed in bfloat16 or wider, within the bound.
No kernel may reach another device: no remote copies, remote signals or barrier semaphores. Data moves between devices by JAX's collectives and lax.ppermute only.
A program may use at most 128 MiB of HBM per device.

v0:
```python
import math

import jax
import jax.numpy as jnp
from jax import lax
from jax.sharding import PartitionSpec as P

HEADS = 20
HD = 128
FD = 4


EPSILON = 0.001


def padded_2(value, sides, width):
    for axis, dim in sides:
        size, length = (lax.axis_size(axis), value.shape[dim])
        up = [(i, (i + 1) % size) for i in range(size)]
        down = [(j, i) for i, j in up]
        last = lax.slice_in_dim(value, length - width, length, axis=dim)
        initial = lax.slice_in_dim(value, 0, width, axis=dim)
        before = lax.ppermute(last, axis, up)
        after = lax.ppermute(initial, axis, down)
        value = jnp.concatenate([before, value, after], axis=dim)
    return value


def softmax_block(query_h, key_h, value_h, score_scale):
    scores = (
        jnp.einsum("qhd,khd->hqk", query_h, key_h, preferred_element_type=jnp.float32) * score_scale
    )
    highest = jnp.max(scores, axis=-1, keepdims=True)
    exponent = jnp.exp(scores - highest)
    denominator = jnp.sum(exponent, axis=-1)
    probability = exponent.astype(jnp.bfloat16)
    summed = jnp.einsum("hqk,khd->qhd", probability, value_h, preferred_element_type=jnp.float32)
    return summed / jnp.transpose(denominator)[:, :, None]


def local(
    queries,
    keys,
    values,
    stream,
    out_weight,
    gate,
    head_shift,
    head_scale,
    head_weight,
    latents,
    step_size,
    intersections,
    ramps,
):
    tok_rows, feat_width = queries.shape
    groups = lax.axis_size("fsdp")
    head_count = HEADS
    score_scale = 1.0 / math.sqrt(HD)
    per_group = head_count // groups
    split_shape = (tok_rows, groups, per_group, HD)
    query_part = lax.all_to_all(
        queries.reshape(split_shape), "fsdp", split_axis=1, concat_axis=0, tiled=True
    )
    key_part = lax.all_to_all(
        keys.reshape(split_shape), "fsdp", split_axis=1, concat_axis=0, tiled=True
    )
    value_part = lax.all_to_all(
        values.reshape(split_shape), "fsdp", split_axis=1, concat_axis=0, tiled=True
    )
    result = softmax_block(query_part[:, 0], key_part[:, 0], value_part[:, 0], score_scale)
    own_heads = result.astype(jnp.bfloat16)[:, None]
    window_rows = own_heads.shape[0]
    own_heads = own_heads.reshape(window_rows, per_group * HD)
    full_columns = lax.all_gather(out_weight, "win", axis=1, tiled=True)
    projected = lax.psum_scatter(
        jnp.dot(own_heads, full_columns, preferred_element_type=jnp.float32).astype(jnp.bfloat16),
        "fsdp",
        scatter_dimension=0,
        tiled=True,
    ).astype(jnp.float32)
    hidden = stream.astype(jnp.float32) + gate * projected
    centre = jnp.mean(hidden, axis=-1, keepdims=True)
    centred = hidden - centre
    variance = jnp.mean(centred * centred, axis=-1, keepdims=True)
    normed = centred / jnp.sqrt(variance + EPSILON)
    modulated = (normed * head_scale + head_shift).astype(jnp.bfloat16)
    velocity = jnp.dot(modulated, head_weight, preferred_element_type=jnp.float32)
    fresh = latents + step_size[0] * velocity.reshape(latents.shape)
    frames_dev = latents.shape[0]
    shared = FD
    padded = padded_2(fresh.astype(jnp.bfloat16), (("win", 0),), shared).astype(fresh.dtype)
    prev_block = padded[:shared]
    next_block = padded[shared + frames_dev :]
    window = lax.axis_index("win")
    win_count = lax.axis_size("win")
    prev_window = (window + win_count - 1) % win_count
    window_ids = jnp.arange(win_count, dtype=jnp.int32)
    over_prev = jnp.sum(jnp.where(window_ids == prev_window, intersections, 0))
    over_next = jnp.sum(jnp.where(window_ids == window, intersections, 0))
    ramp_prev = jnp.sum(
        jnp.where((window_ids == prev_window)[:, None, None], ramps, 0), axis=0
    ).astype(jnp.float32)
    ramp_own = jnp.sum(jnp.where((window_ids == window)[:, None, None], ramps, 0), axis=0).astype(
        jnp.float32
    )
    frame_ids = jnp.arange(frames_dev, dtype=jnp.int32)
    shared_ids = jnp.arange(shared, dtype=jnp.int32)
    inside_prev = frame_ids < over_prev
    select_prev = (
        (shared_ids[None, :] == shared - over_prev + frame_ids[:, None]) & inside_prev[:, None]
    ).astype(jnp.float32)
    prev_aligned = jnp.dot(select_prev, prev_block, precision=lax.Precision.HIGHEST)
    rows_prev = (shared_ids[None, :] == frame_ids[:, None]).astype(jnp.float32)
    ramp_rows_prev = jnp.dot(rows_prev, ramp_prev, precision=lax.Precision.HIGHEST)
    weight_before = ramp_rows_prev[:, 0:1]
    weight_self = ramp_rows_prev[:, 1:2]
    spare_prev = 1.0 - (frame_ids < shared).astype(jnp.float32)[:, None]
    blend_prev = (weight_before * prev_aligned + weight_self * fresh) / (
        weight_before + weight_self + spare_prev
    )
    shifted = frame_ids - (frames_dev - over_next)
    inside_next = shifted >= 0
    select_next = (shared_ids[None, :] == shifted[:, None]).astype(jnp.float32)
    next_aligned = jnp.dot(select_next, next_block, precision=lax.Precision.HIGHEST)
    ramp_rows = jnp.dot(select_next, ramp_own, precision=lax.Precision.HIGHEST)
    weight_mine = ramp_rows[:, 0:1]
    weight_after = ramp_rows[:, 1:2]
    spare = 1.0 - inside_next.astype(jnp.float32)[:, None]
    blend_next = (weight_mine * fresh + weight_after * next_aligned) / (
        weight_mine + weight_after + spare
    )
    return jnp.where(
        inside_prev[:, None], blend_prev, jnp.where(inside_next[:, None], blend_next, fresh)
    )


def solution(mesh):
    in_specs = (
        P(("win", "fsdp"), None),
        P(("win", "fsdp"), None),
        P(("win", "fsdp"), None),
        P(("win", "fsdp"), None),
        P("fsdp", "win"),
        P(),
        P(),
        P(),
        P(),
        P("win", "fsdp"),
        P(),
        P(),
        P(),
    )
    out_specs = P("win", "fsdp")
    return jax.shard_map(local, mesh=mesh, in_specs=in_specs, out_specs=out_specs, check_vma=False)
```

profile of v0, /device:TPU:0, one launch (start us, length us, event | category | flops | bytes accessed | tf_op | source)
XLA Modules:
  0.0 235.3 jit_solution(2147026987415011485)
XLA Ops:
  6.5 0.7 all-gather.2.cloned.1.call-update
  7.3 2.4 %copy.18 = bf16[256,2560]{0,1:T(8,128)(2,1)} copy(bf16[256,2560]{1,0:T(8,128)(2,1)} %param.13) | data formatting | bytes 2621440 | tf_op args[0]
  9.7 4.3 %all-to-all-start = ((bf16[256,4,5,128]{0,3,2,1:T(8,128)(2,1)}), bf16[256,4,5,128]{0,3,2,1:T(8,128)(2,1)S(1)}, u32[]{:S(2)}, u32[]{:S(2)}) async-start(bf16[256,4,5,128]{0,3,2,1:T(8,128)(2,1)} %bitcast.2), calls=%async_computation | async-start | bytes 2621440 | tf_op jit(solution)/shard_map/all_to_all | solution.py:62
  14.0 1.4 copy.20
  15.4 15.8 %all-to-all-done = bf16[256,4,5,128]{0,3,2,1:T(8,128)(2,1)S(1)} async-done(((bf16[256,4,5,128]{0,3,2,1:T(8,128)(2,1)}), bf16[256,4,5,128]{0,3,2,1:T(8,128)(2,1)S(1)}, u32[]{:S(2)}, u32[]{:S(2)}) %all-to-all-start) | async-done | bytes 1310752 | tf_op jit(solution)/shard_map/all_to_all | solution.py:62
  31.2 3.5 %all-to-all-start.1 = ((bf16[256,4,5,128]{0,3,2,1:T(8,128)(2,1)}), bf16[256,4,5,128]{0,3,2,1:T(8,128)(2,1)S(1)}, u32[]{:S(2)}, u32[]{:S(2)}) async-start(bf16[256,4,5,128]{0,3,2,1:T(8,128)(2,1)} %bitcast.49), calls=%async_computation.1 | async-start | bytes 2621440 | tf_op jit(solution)/shard_map/all_to_all | solution.py:65
  34.7 2.4 %copy.22 = bf16[256,2560]{0,1:T(8,128)(2,1)} copy(bf16[256,2560]{1,0:T(8,128)(2,1)} %param.15) | data formatting | bytes 2621440 | tf_op args[2]
  37.2 14.8 %all-to-all-done.1 = bf16[256,4,5,128]{0,3,2,1:T(8,128)(2,1)S(1)} async-done(((bf16[256,4,5,128]{0,3,2,1:T(8,128)(2,1)}), bf16[256,4,5,128]{0,3,2,1:T(8,128)(2,1)S(1)}, u32[]{:S(2)}, u32[]{:S(2)}) %all-to-all-start.1) | async-done | bytes 1310752 | tf_op jit(solution)/shard_map/all_to_all | solution.py:65
  52.0 4.3 %all-to-all-start.2 = ((bf16[256,4,5,128]{0,3,2,1:T(8,128)(2,1)}), bf16[256,4,5,128]{0,3,2,1:T(8,128)(2,1)}, u32[]{:S(2)}, u32[]{:S(2)}) async-start(bf16[256,4,5,128]{0,3,2,1:T(8,128)(2,1)} %bitcast.48), calls=%async_computation.2 | async-start | bytes 2621440 | tf_op jit(solution)/shard_map/all_to_all | solution.py:68
  56.3 0.8 copy.19
  57.1 1.8 copy.21
  58.9 14.7 %all-to-all-done.2 = bf16[256,4,5,128]{0,3,2,1:T(8,128)(2,1)} async-done(((bf16[256,4,5,128]{0,3,2,1:T(8,128)(2,1)}), bf16[256,4,5,128]{0,3,2,1:T(8,128)(2,1)}, u32[]{:S(2)}, u32[]{:S(2)}) %all-to-all-start.2) | async-done | bytes 1310752 | tf_op jit(solution)/shard_map/all_to_all | solution.py:68
  73.6 3.4 %copy.23 = bf16[4,256,1,5,128]{1,0,4,3,2:T(4,128)(2,1)} copy(bf16[4,256,1,5,128]{1,4,3,0,2:T(8,128)(2,1)} %bitcast.12) | data formatting | bytes 2621440 | tf_op jit(solution)/shard_map/all_to_all | solution.py:68
  77.0 3.7 %squeeze.15 = bf16[1024,5,128]{0,2,1:T(8,128)(2,1)} reshape(bf16[4,256,1,5,128]{1,0,4,3,2:T(4,128)(2,1)} %copy.23) | data formatting | bytes 2621440 | tf_op jit(solution)/shard_map/squeeze | solution.py:71
  80.6 2.9 %multiply_reduce_fusion = (f32[5,1024]{1,0:T(8,128)S(1)}, f32[5,1024,1024]{1,2,0:T(8,128)S(1)}) fusion(bf16[1024,5,128]{2,0,1:T(8,128)(2,1)S(1)} %bitcast.44, bf16[1024,5,128]{2,0,1:T(8,128)(2,1)S(1)} %bitcast.45), kind=kOutput, calls=%fused_computation.1 | convolution fusion | flops 1352657920 | bytes 23613440 | tf_op jit(solution)/shard_map/qhd,khd->hqk/dot_general | solution.py:31
  83.5 3.7 %fusion = f32[5,1024]{1,0:T(8,128)S(1)} fusion(f32[5,1024,1024]{1,2,0:T(8,128)S(1)} %get-tuple-element.20, f32[5,1024]{1,0:T(8,128)S(1)} %get-tuple-element.19), kind=kLoop, calls=%fused_computation.2 | loop fusion | flops 15723520 | bytes 21012480 | tf_op jit(solution)/shard_map/reduce_sum | solution.py:35
  87.2 3.7 %copy-done.1 = f32[5,1024,1024]{1,2,0:T(8,128)} copy-done((f32[5,1024,1024]{1,2,0:T(8,128)}, f32[5,1024,1024]{1,2,0:T(8,128)S(1)}, u32[]{:S(2)}) %copy-start.1) | copy-done | bytes 20971544
  91.0 11.2 %fusion.7 = bf16[1024,5,128]{0,2,1:T(8,128)(2,1)S(1)} fusion(bf16[1024,5,128]{0,2,1:T(8,128)(2,1)S(1)} %copy-done.6, f32[5,1024,1024]{1,2,0:T(8,128)} %copy-done.1, f32[5,1024]{1,0:T(8,128)S(1)} %get-tuple-element.19, f32[1024,5]{0,1:T(8,128)S(1)} %bitcast.50), kind=kOutput, calls=%fused_computation.13 | convolution fusion | flops 1359216640 | bytes 23633920 | tf_op jit(solution)/shard_map/hqk,khd->qhd/dot_general | solution.py:37
  102.2 12.1 %all-gather.2.cloned.1.call-done = bf16[640,5120]{1,0:T(8,128)(2,1)} async-done(((bf16[640,640]{1,0:T(8,128)(2,1)}), bf16[640,5120]{1,0:T(8,128)(2,1)}) %all-gather.2.cloned.1.call-update) | async-done | bytes 6553616 | tf_op jit(solution)/shard_map/all_gather | solution.py:75
  114.3 13.8 %convolution_convert_fusion = bf16[1024,5120]{1,0:T(8,128)(2,1)} fusion(bf16[1024,640]{0,1:T(8,128)(2,1)S(1)} %bitcast.51, bf16[640,5120]{1,0:T(8,128)(2,1)} %all-gather.2.cloned.1.call-done), kind=kOutput, calls=%fused_computation.7 | convolution fusion | flops 6716129280 | bytes 18350080 | tf_op jit(solution)/shard_map/dot_general | solution.py:77
  129.0 0.7 select_reduce_fusion.3
  130.9 0.6 iota_compare_fusion.8
  131.6 0.2 select_reduce_fusion.1
  131.8 0.2 fusion.18
  132.2 78.6 %reduce-scatter.2.cloned.1.call-done = bf16[256,5120]{1,0:T(8,128)(2,1)} async-done(((bf16[1024,5120]{1,0:T(8,128)(2,1)}), bf16[256,5120]{1,0:T(8,128)(2,1)}) %reduce-scatter.2.cloned.1.call-update) | async-done | bytes 2621456 | tf_op jit(solution)/shard_map/reduce_scatter | solution.py:76
  210.9 2.8 %fusion.6 = f32[256]{0:T(256)S(1)} fusion(bf16[256,5120]{1,0:T(8,128)(2,1)} %reduce-scatter.2.cloned.1.call-done, bf16[256,5120]{1,0:T(8,128)(2,1)S(1)} %copy-done.2, f32[5120]{0:T(1024)S(1)} %copy-done.7), kind=kLoop, calls=%fused_computation.11 | loop fusion | flops 6553344 | bytes 5264384 | tf_op jit(solution)/shard_map/reduce_sum | solution.py:83
  213.7 1.3 multiply_reduce_fusion.1
  215.1 1.7 fusion.17
  217.0 4.3 %collective-permute-start.1 = (bf16[4,1024]{1,0:T(4,128)(2,1)S(1)}, bf16[4,1024]{1,0:T(4,128)(2,1)S(1)}, u32[]{:S(2)}, u32[]{:S(2)}) collective-permute-start(bf16[4,1024]{1,0:T(4,128)(2,1)S(1)} %get-tuple-element.12), channel_id=1, source_target_pairs={{4,0},{8,4},{12,8},{16,12},{20,16},{24,20},{28,24},{0,28},{5,1},{9... | collective-permute-start | bytes 24584 | tf_op jit(solution)/shard_map/ppermute | solution.py:24
  221.3 1.4 collective-permute-done.1
  222.9 4.8 %collective-permute-done = bf16[4,1024]{1,0:T(4,128)(2,1)S(1)} collective-permute-done((bf16[4,1024]{1,0:T(4,128)(2,1)S(1)}, bf16[4,1024]{1,0:T(4,128)(2,1)S(1)}, u32[]{:S(2)}, u32[]{:S(2)}) %collective-permute-start) | collective-permute-done | bytes 8224 | tf_op jit(solution)/shard_map/ppermute | solution.py:23
  227.6 0.8 fusion.16
  (43 shorter events, 0.8 us)
Async XLA Ops:
  6.5 208.5 %copy-start = (bf16[5120,64]{0,1:T(8,128)(2,1)S(1)}, bf16[5120,64]{0,1:T(8,128)(2,1)}, u32[]{:S(2)}) copy-start(bf16[5120,64]{0,1:T(8,128)(2,1)} %param.21) | copy-start | bytes 1966084
  6.5 7.4 %copy-start.5 = (bf16[256,2560]{1,0:T(8,128)(2,1)S(1)}, bf16[256,2560]{1,0:T(8,128)(2,1)}, u32[]{:S(2)}) copy-start(bf16[256,2560]{1,0:T(8,128)(2,1)} %param.14) | copy-start | bytes 3932164
  6.5 107.7 %all-gather.2.cloned.1.call-start = ((), (), s32[]{:S(2)}) async-start(), calls=%async_computation.4 | async-start | bytes 7372800 | tf_op jit(solution)/shard_map/all_gather | solution.py:75
  9.7 21.5 %all-to-all-start = ((bf16[256,4,5,128]{0,3,2,1:T(8,128)(2,1)}), bf16[256,4,5,128]{0,3,2,1:T(8,128)(2,1)S(1)}, u32[]{:S(2)}, u32[]{:S(2)}) async-start(bf16[256,4,5,128]{0,3,2,1:T(8,128)(2,1)} %bitcast.2), calls=%async_computation | async-start | bytes 2621440 | tf_op jit(solution)/shard_map/all_to_all | solution.py:62
  31.2 20.8 %all-to-all-start.1 = ((bf16[256,4,5,128]{0,3,2,1:T(8,128)(2,1)}), bf16[256,4,5,128]{0,3,2,1:T(8,128)(2,1)S(1)}, u32[]{:S(2)}, u32[]{:S(2)}) async-start(bf16[256,4,5,128]{0,3,2,1:T(8,128)(2,1)} %bitcast.49), calls=%async_computation.1 | async-start | bytes 2621440 | tf_op jit(solution)/shard_map/all_to_all | solution.py:65
  52.0 4.4 %copy-start.4 = (bf16[256,4,5,128]{0,3,2,1:T(8,128)(2,1)}, bf16[256,4,5,128]{0,3,2,1:T(8,128)(2,1)S(1)}, u32[]{:S(2)}) copy-start(bf16[256,4,5,128]{0,3,2,1:T(8,128)(2,1)S(1)} %all-to-all-done.1) | copy-start | bytes 3932164
  52.0 21.6 %all-to-all-start.2 = ((bf16[256,4,5,128]{0,3,2,1:T(8,128)(2,1)}), bf16[256,4,5,128]{0,3,2,1:T(8,128)(2,1)}, u32[]{:S(2)}, u32[]{:S(2)}) async-start(bf16[256,4,5,128]{0,3,2,1:T(8,128)(2,1)} %bitcast.48), calls=%async_computation.2 | async-start | bytes 2621440 | tf_op jit(solution)/shard_map/all_to_all | solution.py:68
  56.3 154.6 %reduce-scatter.2.cloned.1.call-start = ((), (), s32[]{:S(2)}) async-start(), calls=%async_computation.5 | async-start | bytes 13107200 | tf_op jit(solution)/shard_map/reduce_scatter | solution.py:76
  83.5 7.4 %copy-start.1 = (f32[5,1024,1024]{1,2,0:T(8,128)}, f32[5,1024,1024]{1,2,0:T(8,128)S(1)}, u32[]{:S(2)}) copy-start(f32[5,1024,1024]{1,2,0:T(8,128)S(1)} %get-tuple-element.20) | copy-start | bytes 62914564
  83.5 7.4 %copy-start.6 = (bf16[1024,5,128]{0,2,1:T(8,128)(2,1)S(1)}, bf16[1024,5,128]{0,2,1:T(8,128)(2,1)}, u32[]{:S(2)}) copy-start(bf16[1024,5,128]{0,2,1:T(8,128)(2,1)} %squeeze.15) | copy-start | bytes 3932164
  128.1 0.9 copy-start.10
  128.1 3.5 %copy-start.9 = (s32[8,4,2]{0,2,1:T(2,128)S(1)}, s32[8,4,2]{0,2,1:T(2,128)}, u32[]{:S(2)}) copy-start(s32[8,4,2]{0,2,1:T(2,128)} %param.25) | copy-start | bytes 772
  128.1 82.8 %copy-start.2 = (bf16[256,5120]{1,0:T(8,128)(2,1)S(1)}, bf16[256,5120]{1,0:T(8,128)(2,1)}, u32[]{:S(2)}) copy-start(bf16[256,5120]{1,0:T(8,128)(2,1)} %param.16) | copy-start | bytes 7864324
  128.1 82.8 %copy-start.7 = (f32[5120]{0:T(1024)S(1)}, f32[5120]{0:T(1024)}, u32[]{:S(2)}) copy-start(f32[5120]{0:T(1024)} %param.18) | copy-start | bytes 61444
  132.2 82.8 %copy-start.11 = (f32[5120]{0:T(1024)S(1)}, f32[5120]{0:T(1024)}, u32[]{:S(2)}) copy-start(f32[5120]{0:T(1024)} %param.19) | copy-start | bytes 61444
  132.2 82.8 %copy-start.12 = (f32[5120]{0:T(1024)S(1)}, f32[5120]{0:T(1024)}, u32[]{:S(2)}) copy-start(f32[5120]{0:T(1024)} %param.20) | copy-start | bytes 61444
  210.9 2.8 %copy-start.3 = (bf16[256,5120]{1,0:T(8,128)(2,1)S(1)}, bf16[256,5120]{1,0:T(8,128)(2,1)}, u32[]{:S(2)}) copy-start(bf16[256,5120]{1,0:T(8,128)(2,1)} %reduce-scatter.2.cloned.1.call-done) | copy-start | bytes 7864324
  215.0 1.9 copy-start.8
  217.0 5.7 %collective-permute-start.1 = (bf16[4,1024]{1,0:T(4,128)(2,1)S(1)}, bf16[4,1024]{1,0:T(4,128)(2,1)S(1)}, u32[]{:S(2)}, u32[]{:S(2)}) collective-permute-start(bf16[4,1024]{1,0:T(4,128)(2,1)S(1)} %get-tuple-element.12), channel_id=1, source_target_pairs={{4,0},{8,4},{12,8},{16,12},{20,16},{24,20},{28,24},{0,28},{5,1},{9... | collective-permute-start | bytes 24584 | tf_op jit(solution)/shard_map/ppermute | solution.py:24
  221.3 6.3 %collective-permute-start = (bf16[4,1024]{1,0:T(4,128)(2,1)S(1)}, bf16[4,1024]{1,0:T(4,128)(2,1)S(1)}, u32[]{:S(2)}, u32[]{:S(2)}) collective-permute-start(bf16[4,1024]{1,0:T(4,128)(2,1)S(1)} %get-tuple-element.11), channel_id=1, source_target_pairs={{0,4},{4,8},{8,12},{12,16},{16,20},{20,24},{24,28},{28,0},{1,5},{5... | collective-permute-start | bytes 24584 | tf_op jit(solution)/shard_map/ppermute | solution.py:23
Sparse Core Ops, SparseCore 0:
  9.6 104.6 all-gather.1
  128.3 82.5 reduce-scatter.1
where the time goes:
time: 236 us; the launch traced here: 235 us
  waiting for transfers between devices  143 us (61%)
  matrix products  31 us (13%)
  local copies, waits for them, and re-layouts  19.9 us (8%)
  starting transfers between devices  16.5 us (7%)
  between operations  15.7 us (7%)
  other arithmetic  9.4 us (4%)
    reduce_scatter x1, waiting for transfers between devices, local(): lax.psum_scatter(jnp.dot(own_heads, full_columns, preferred_element_type=...  78.6 us
    all_to_all x1, waiting for transfers between devices, local(): lax.all_to_all(queries.reshape(split_shape), 'fsdp', split_axis=1, concat...  15.8 us
    all_to_all x1, waiting for transfers between devices, local(): lax.all_to_all(keys.reshape(split_shape), 'fsdp', split_axis=1, concat_ax...  14.8 us
    all_to_all x1, waiting for transfers between devices, local(): lax.all_to_all(values.reshape(split_shape), 'fsdp', split_axis=1, concat_...  14.7 us
    dot_general x1, matrix products, local(): jnp.dot(own_heads, full_columns, preferred_element_type=jnp.float32)  13.8 us
    all_gather x1, waiting for transfers between devices, local(): full_columns = lax.all_gather(out_weight, 'win', axis=1, tiled=True)  12.1 us
    dot_general x1, matrix products, softmax_block(): jnp.einsum('hqk,khd->qhd', probability, value_h, preferred_element_type=j...  11.2 us
    unnamed x29, local copies, waits for them, and re-layouts  10.1 us
  transfers between devices with their start and end apart: 7, of which 7 were waited for; matrix products, arithmetic and copies ran while one was open for 15% of the time, Pallas kernels for 0%

commit v1 on v0

v1 whole, which is shorter than its diff:
```python
import functools
import math

import jax
import jax.numpy as jnp
from jax import lax
from jax.experimental import pallas as pl
from jax.experimental.pallas import tpu as pltpu
from jax.sharding import PartitionSpec as P


HD = 128
FD = 4
EPSILON = 0.001
LANES = 128


def swap(value, axis, bits):
    size = lax.axis_size(axis)
    return lax.ppermute(value, axis, [(i, i ^ bits) for i in range(size)])


def line_move(value, moves):
    pairs = [(2 * a + p, 2 * b + p) for a, b in moves for p in range(2)]
    return lax.ppermute(value, "win", pairs)


def attend_kernel(score_scale, ids, q_ref, k_ref, v_ref, mate_ref, far_ref, diag_ref, out_ref):
    keys = [k_ref[...], mate_ref[0, 1], far_ref[0], diag_ref[0]]
    values = [v_ref[...], mate_ref[0, 2], far_ref[1], diag_ref[1]]
    factor = score_scale * math.log2(math.e)
    for half, query in enumerate((q_ref[...], mate_ref[0, 0])):
        scores = [
            lax.dot_general(query, k, (((1,), (1,)), ((), ())), preferred_element_type=jnp.float32)
            for k in keys
        ]
        peaks = [jnp.max(s, axis=-1, keepdims=True) for s in scores]
        highest = functools.reduce(jnp.maximum, peaks)
        total = None
        summed = None
        for s, v in zip(scores, values):
            exponent = jnp.exp2((s - highest) * factor)
            part = jnp.sum(exponent, axis=-1, keepdims=True)
            prod = jnp.dot(exponent.astype(jnp.bfloat16), v, preferred_element_type=jnp.float32)
            total = part if total is None else total + part
            summed = prod if summed is None else summed + prod
        out_ref[half] = (summed / total).astype(jnp.bfloat16)


def attend(ids, queries, keys, values, mate, far, diag, part, first, count, heads):
    rows = queries.shape[0]
    wide = pl.BlockSpec((rows, HD), lambda h, ids: (0, ids[part] * heads + first + h))
    narrow = pl.BlockSpec((2, rows, HD), lambda h, ids: (0, 0, h))
    return pl.pallas_call(
        functools.partial(attend_kernel, 1.0 / math.sqrt(HD)),
        grid_spec=pltpu.PrefetchScalarGridSpec(
            num_scalar_prefetch=1,
            grid=(count,),
            in_specs=[wide] * 3
            + [pl.BlockSpec((1, 3, rows, HD), lambda h, ids: (part, 0, 0, first + h))]
            + [narrow] * 2,
            out_specs=narrow,
        ),
        out_shape=jax.ShapeDtypeStruct((2, rows, count * HD), jnp.bfloat16),
        cost_estimate=pl.CostEstimate(
            flops=32 * rows * rows * HD * count,
            bytes_accessed=24 * rows * HD * count,
            transcendentals=8 * rows * rows * count,
        ),
    )(ids, queries, keys, values, mate, far, diag)


def fetch_weights(picks, ids, sources, held, sems):
    copies = []
    at = 0
    for j, pick in enumerate(picks):
        for c in range(pick):
            copy = pltpu.make_async_copy(sources[at + c], held.at[j], sems.at[j])
            if pick == 1:
                pl.when(pl.program_id(0) == 0)(copy.start)
            else:
                pl.when((pl.program_id(0) == 0) & (ids[j] == c))(copy.start)
        copies.append(pltpu.make_async_copy(sources[at], held.at[j], sems.at[j]))
        at += pick
    return copies


def projected(att, held, slot, depth):
    total = None
    start = 0
    for part in att:
        cols = part.shape[-1]
        weight = held[2 * slot + start // depth, pl.ds(start % depth, cols), :]
        term = jnp.dot(part[0], weight, preferred_element_type=jnp.float32)
        total = term if total is None else total + term
        start += cols
    return total


def give_kernel(picks, chunks, ids, *refs):
    att = refs[: 2 * chunks]
    sources = refs[2 * chunks : 2 * chunks + sum(picks)]
    give_ref, held, sems = refs[2 * chunks + sum(picks) :]
    depth = held.shape[1]
    copies = fetch_weights(picks, ids, sources, held, sems)
    for b in range(len(picks) // 2):
        @pl.when(pl.program_id(0) == b)
        def _():
            copies[2 * b].wait()
            copies[2 * b + 1].wait()
            for w in range(2):
                part = projected(att[w * chunks : (w + 1) * chunks], held, b, depth)
                give_ref[0, w] = part.astype(jnp.bfloat16)


def weight_specs(att, half, sources):
    spec = lambda v: pl.BlockSpec((1,) + v.shape[1:], lambda b, ids: (half, 0, 0))
    return [spec(v) for v in att] + [pl.BlockSpec(memory_space=pl.ANY)] * sum(
        len(s) for s in sources
    )


def give(ids, att, sources):
    rows = att[0].shape[1]
    depth, span = sources[0][0].shape
    slots = len(sources)
    return pl.pallas_call(
        functools.partial(give_kernel, tuple(len(s) for s in sources), len(att) // 2),
        grid_spec=pltpu.PrefetchScalarGridSpec(
            num_scalar_prefetch=1,
            grid=(slots // 2,),
            in_specs=weight_specs(att, 1, sources),
            out_specs=pl.BlockSpec((1, 2, rows, span), lambda b, ids: (b, 0, 0, 0)),
            scratch_shapes=[
                pltpu.VMEM((slots, depth, span), jnp.bfloat16),
                pltpu.SemaphoreType.DMA((slots,)),
            ],
        ),
        out_shape=jax.ShapeDtypeStruct((slots // 2, 2, rows, span), jnp.bfloat16),
        cost_estimate=pl.CostEstimate(
            flops=4 * rows * depth * span * slots,
            bytes_accessed=8 * rows * depth + 2 * slots * depth * span,
            transcendentals=0,
        ),
    )(ids, *att, *(o for s in sources for o in s))


def tally_kernel(picks, chunks, first, ids, *refs):
    att = refs[: 2 * chunks]
    sources = refs[2 * chunks : 2 * chunks + sum(picks)]
    got_ref, own_ref, other_ref, gate_ref, scale_ref, head_ref, old_ref, out_ref, held, sems = refs[
        2 * chunks + sum(picks) :
    ]
    depth = held.shape[1]
    rows = own_ref.shape[0]
    head = head_ref[0]
    chans = head.shape[1]
    copies = fetch_weights(picks, ids, sources, held, sems)
    for b in range(len(picks) // 2):
        @pl.when(pl.program_id(0) == b)
        def _():
            copies[2 * b].wait()
            copies[2 * b + 1].wait()
            for w, stream in enumerate((own_ref[...], other_ref[0])):
                proj = projected(att[w * chunks : (w + 1) * chunks], held, b, depth)
                proj = proj + got_ref[0, w].astype(jnp.float32)
                hidden = stream.astype(jnp.float32) + gate_ref[0] * proj
                at = pl.ds(w * rows, rows)
                fresh = first and b == 0
                if fresh:
                    centre = jnp.mean(hidden, axis=-1, keepdims=True)
                else:
                    old = (old_ref if b == 0 else out_ref)[at, :]
                    centre = old[:, chans : chans + 1]
                moved = hidden - centre
                dots = jnp.dot(
                    (moved * scale_ref[0]).astype(jnp.bfloat16),
                    head,
                    preferred_element_type=jnp.float32,
                )
                one = jnp.sum(moved, axis=-1, keepdims=True)
                two = jnp.sum(moved * moved, axis=-1, keepdims=True)
                if not fresh:
                    dots = dots + old[:, :chans]
                    one = one + old[:, chans + 1 : chans + 2]
                    two = two + old[:, chans + 2 : chans + 3]
                out_ref[at, :chans] = dots
                lane = lax.broadcasted_iota(jnp.int32, (rows, out_ref.shape[1] - chans), 1)
                out_ref[at, chans:] = jnp.where(
                    lane == 0, centre, jnp.where(lane == 1, one, jnp.where(lane == 2, two, 0.0))
                )


def tally(ids, att, sources, got, own, other, gate, scale, head, stats):
    rows = att[0].shape[1]
    depth, span = sources[0][0].shape
    chans = head.shape[2]
    slots = len(sources)
    by_block = lambda shape: pl.BlockSpec((1,) + shape, lambda b, ids: (ids[slots + b], 0, 0))
    lanes = chans + LANES - chans % LANES
    first = stats is None
    if first:
        stats = jnp.zeros((8, LANES), jnp.float32)
    return pl.pallas_call(
        functools.partial(tally_kernel, tuple(len(s) for s in sources), len(att) // 2, first),
        grid_spec=pltpu.PrefetchScalarGridSpec(
            num_scalar_prefetch=1,
            grid=(slots // 2,),
            in_specs=weight_specs(att, 0, sources)
            + [
                pl.BlockSpec((1, 2, rows, span), lambda b, ids: (b, 0, 0, 0)),
                pl.BlockSpec((rows, span), lambda b, ids: (0, ids[slots + b])),
                pl.BlockSpec((1, rows, span), lambda b, ids: (ids[slots + slots // 2 + b], 0, 0)),
            ]
            + [by_block((1, span))] * 2
            + [
                by_block((span, chans)),
                pl.BlockSpec(stats.shape, lambda b, ids: (0, 0)),
            ],
            out_specs=pl.BlockSpec((2 * rows, lanes), lambda b, ids: (0, 0)),
            scratch_shapes=[
                pltpu.VMEM((slots, depth, span), jnp.bfloat16),
                pltpu.SemaphoreType.DMA((slots,)),
            ],
        ),
        out_shape=jax.ShapeDtypeStruct((2 * rows, lanes), jnp.float32),
        cost_estimate=pl.CostEstimate(
            flops=4 * rows * depth * span * slots,
            bytes_accessed=8 * rows * depth + 2 * slots * depth * span,
            transcendentals=0,
        ),
    )(ids, *att, *(o for s in sources for o in s), got, own, other, gate, scale, head, stats)


def after(value, *marks):
    return lax.optimization_barrier((value,) + marks)[0]


def blend_weights(intersections, ramps, frames):
    window = lax.axis_index("win")
    count = lax.axis_size("win")
    prev_window = (window + count - 1) % count
    over_prev = lax.dynamic_index_in_dim(intersections, prev_window, keepdims=False)
    over_next = lax.dynamic_index_in_dim(intersections, window, keepdims=False)
    ramp_prev = lax.dynamic_index_in_dim(ramps, prev_window, keepdims=False).astype(jnp.float32)
    ramp_own = lax.dynamic_index_in_dim(ramps, window, keepdims=False).astype(jnp.float32)
    frame = jnp.arange(frames, dtype=jnp.int32)[:, None]
    shared = jnp.arange(FD, dtype=jnp.int32)[None, :]
    share_prev = ramp_prev / (ramp_prev[:, 0:1] + ramp_prev[:, 1:2])
    share_own = ramp_own / (ramp_own[:, 0:1] + ramp_own[:, 1:2])
    inside_prev = frame < over_prev
    at_prev = inside_prev & (shared == frame)
    take_prev = inside_prev & (shared == FD - over_prev + frame)
    weight_before = jnp.sum(jnp.where(at_prev, share_prev[None, :, 0], 0.0), axis=1, keepdims=True)
    self_prev = jnp.sum(jnp.where(at_prev, share_prev[None, :, 1], 0.0), axis=1, keepdims=True)
    place = frame - (frames - over_next)
    inside_next = (place >= 0) & ~inside_prev
    at_next = inside_next & (shared == place)
    self_next = jnp.sum(jnp.where(at_next, share_own[None, :, 0], 0.0), axis=1, keepdims=True)
    coef_prev = jnp.where(take_prev, weight_before, 0.0)
    coef_next = jnp.where(at_next, share_own[None, :, 1], 0.0)
    own = jnp.where(inside_prev, self_prev, jnp.where(inside_next, self_next, 1.0))
    return own, coef_prev, coef_next


def local(
    queries,
    keys,
    values,
    stream,
    out_weight,
    gate,
    head_shift,
    head_scale,
    head_weight,
    latents,
    step_size,
    intersections,
    ramps,
):
    rows, feat = queries.shape
    groups = lax.axis_size("fsdp")
    count = lax.axis_size("win")
    line = count // 2
    width = out_weight.shape[1]
    model = stream.shape[1]
    chans = head_weight.shape[1]
    cols = feat // groups
    heads = cols // HD
    window = lax.axis_index("win")
    member = lax.axis_index("fsdp")
    z = window // 2
    parity = window % 2
    regroup = width % LANES != 0 or line != 4
    blocks = line
    if regroup:
        blocks = max(b for b in (1, 2, 4) if (model // 2) % (b * LANES) == 0)
    span = model // 2 // blocks

    def group(value, bits):
        return lax.dynamic_slice(value, (0, (member ^ bits) * cols), (rows, cols))

    def pack(bits, *arrays):
        return jnp.stack([group(v, bits) for v in arrays])

    ids = jnp.stack([member, member ^ 2]).astype(jnp.int32)
    if regroup:
        sets = [[2 * a + p for a in range(line)] for p in range(2)]
        full = lax.all_gather(out_weight, "win", axis=1, tiled=True, axis_index_groups=sets)
        near = [[full[:, r * span : (r + 1) * span]] for r in range(blocks)]
        far = [[swap(b[0], "fsdp", 2)] for b in near]
        picks = [0] * blocks
        half_first = lambda v: jnp.swapaxes(v.reshape((line, 2, width) + v.shape[1:]), 0, 1)
        places = [(parity * blocks + r, r) for r in range(blocks)]
        ordered = half_first(stream.T).reshape(model, rows).T
        sent = [(1 - parity) * blocks + r for r in range(blocks)]
    else:
        down = [(a + 1, a) for a in range(line - 1)]
        up = [(a, a + 1) for a in range(line - 1)]
        on_down = [(a - 1, a - 2) for a in range(2, line)]
        on_up = [(a + 1, a + 2) for a in range(line - 2)]
        far_w = swap(out_weight, "fsdp", 2)
        near_up = line_move(out_weight, up)
        near_down = line_move(out_weight, down)
        half_first = lambda v: v
        ordered = stream
        sent = [2 * r + 1 - parity for r in range(blocks)]
    sizes = [(0, 0, heads), (1, 0, (heads + 1) // 2), (1, (heads + 1) // 2, heads // 2)]

    def sends(chunk, mark):
        part, first, size = chunk
        at = slice(first * HD, (first + size) * HD)
        direct = pack(2 if part == 0 else 0, keys, values)[:, :, at]
        cross = pack(3 if part == 0 else 1, keys, values)[:, :, at]
        if mark is not None:
            direct, cross = after((direct, cross), mark)
        return swap(direct, "fsdp", 2), swap(cross, "fsdp", 3)

    kv0 = sends(sizes[0], None)
    mate = swap(
        jnp.stack([pack(1, queries, keys, values), pack(3, queries, keys, values)]), "fsdp", 1
    )
    other_stream = swap(
        jnp.stack([lax.dynamic_slice(ordered, (0, b * span), (rows, span)) for b in sent]), "win", 1
    )
    if not regroup:
        up2 = line_move(near_up, on_up)
        down2 = line_move(near_down, on_down)
        near2 = jnp.where(z >= 2, up2, down2)
        edge = line_move(near2, [(2, 3), (1, 0)])
        far_up = line_move(far_w, up)
        far_down = line_move(far_w, down)
    kv1 = sends(sizes[1], kv0)

    def run(chunk, kv):
        return attend(ids, queries, keys, values, mate, *kv, *chunk, heads)

    att0 = run(sizes[0], kv0)
    att0_x = swap(att0, "win", 1)
    kv2 = sends(sizes[2], kv1)
    att1 = run(sizes[1], kv1)
    att1_x = swap(att1, "win", 1)
    if not regroup:
        ends = [
            ((w * groups + f), (w * groups + (f ^ 2)))
            for w in range(count)
            if w // 2 in (0, line - 1)
            for f in range(groups)
        ]
        edge, far_up, far_down = after((edge, far_up, far_down), att1)
        far_edge = lax.ppermute(edge, ("win", "fsdp"), ends)
        far_up2 = line_move(far_up, on_up)
        far_down2 = line_move(far_down, on_down)
        at_top = (z == line - 1).astype(jnp.int32)
        at_end = ((z == line - 1) | (z == 0)).astype(jnp.int32)
        upper = (z >= 2).astype(jnp.int32)
        near = [[out_weight], [near_down, near_up], [near2], [near_up, edge]]
        far = [[far_w], [far_down, far_up], [far_down2, far_up2], [far_up, far_edge]]
        picks = [(0, 0), (at_top, at_top), (0, upper), (at_end, at_end)]
        steps = [0, jnp.where(z == line - 1, 3, 1), 2, jnp.where(z == line - 1, 1, 3)]
        places = [(2 * ((z + r) % line) + parity, (z + r) % line) for r in steps]
    else:
        picks = [(0, 0)] * blocks
    att2 = run(sizes[2], kv2)
    att2_x = swap(att2, "win", 1)
    att = (att0, att1, att2, att0_x, att1_x, att2_x)

    gate_b = half_first(gate).reshape(2 * blocks, 1, span)
    scale_b = half_first(head_scale).reshape(2 * blocks, 1, span)
    head_b = half_first(head_weight).reshape(2 * blocks, span, chans)
    each = 2 if blocks % 2 == 0 else 1
    calls = []
    for first in range(0, blocks, each):
        now = range(first, first + each)
        sources = [s[b] for b in now for s in (near, far)]
        chosen = [p for b in now for p in picks[b]]
        chosen += [places[b][i] for i in range(2) for b in now]
        chosen = jnp.stack([jnp.asarray(c, jnp.int32) for c in chosen])
        sent = give(chosen, att, sources)
        calls.append((chosen, sources, swap(sent, "fsdp", 1)))
    stats = None
    for chosen, sources, got in calls:
        stats = tally(
            chosen, att, sources, got, ordered, other_stream, gate_b, scale_b, head_b, stats
        )

    mine = stats[:rows]
    theirs = swap(stats[rows:], "win", 1)
    head_f = head_weight.astype(jnp.float32)
    scaled = (head_scale[:, None] * head_f).reshape(line, 2, width, chans)
    per_half = jnp.sum(scaled, axis=(0, 2))
    own_cw = lax.dynamic_index_in_dim(per_half, parity, keepdims=True)
    their_cw = lax.dynamic_index_in_dim(per_half, 1 - parity, keepdims=True)
    offset = jnp.sum(head_shift[:, None] * head_f, axis=0, keepdims=True)
    half = model // 2

    def fields(s):
        return s[:, :chans], s[:, chans : chans + 1], s[:, chans + 1 : chans + 2], s[:, chans + 2 : chans + 3]

    dot_a, mid_a, one_a, two_a = fields(mine)
    dot_b, mid_b, one_b, two_b = fields(theirs)
    centre = (one_a + one_b) / model + 0.5 * (mid_a + mid_b)
    da = centre - mid_a
    db = centre - mid_b
    square = (two_a - 2.0 * da * one_a + half * da * da) + (two_b - 2.0 * db * one_b + half * db * db)
    inverse = 1.0 / jnp.sqrt(square / model + EPSILON)
    velocity = (dot_a + dot_b - da * own_cw - db * their_cw) * inverse + offset
    fresh = latents + step_size[0] * velocity.reshape(latents.shape)
    frames = latents.shape[0]

    up = [(i, (i + 1) % count) for i in range(count)]
    down = [(j, i) for i, j in up]
    sent = fresh.astype(jnp.bfloat16)
    tail = lax.ppermute(sent[frames - FD :], "win", up).astype(jnp.float32)
    start = lax.ppermute(sent[:FD], "win", down).astype(jnp.float32)
    own, coef_prev, coef_next = blend_weights(intersections, ramps, frames)
    out = own * fresh
    for j in range(FD):
        out = out + coef_prev[:, j : j + 1] * tail[j : j + 1]
        out = out + coef_next[:, j : j + 1] * start[j : j + 1]
    return out


def solution(mesh):
    in_specs = (
        P(("win", "fsdp"), None),
        P(("win", "fsdp"), None),
        P(("win", "fsdp"), None),
        P(("win", "fsdp"), None),
        P("fsdp", "win"),
        P(),
        P(),
        P(),
        P(),
        P("win", "fsdp"),
        P(),
        P(),
        P(),
    )
    out_specs = P("win", "fsdp")

    return jax.shard_map(local, mesh=mesh, in_specs=in_specs, out_specs=out_specs, check_vma=False)
```

time: 236 us -> 201 us (0.85)
  waiting for transfers between devices: 143 us -> 70.5 us
  Pallas kernels: 0 us -> 51.2 us
  matrix products: 31 us -> 0 us
  starting transfers between devices: 16.5 us -> 38.7 us
  between operations: 15.7 us -> 2.48 us
  other arithmetic: 9.4 us -> 20 us
  local copies, waits for them, and re-layouts: 19.9 us -> 17.1 us
    reduce_scatter x1 -> x0, waiting for transfers between devices: 78.6 us -> none  [local(): lax.psum_scatter(jnp.dot(own_heads, full_columns, preferred_element_type=...]
    ppermute x2 -> x27, waiting for transfers between devices: 6.14 us -> 70.5 us  [the longest x15 69.1 us: swap(): return lax.ppermute(value, axis, [(i, i ^ bits) for i in range(size)])]
    pallas_call x0 -> x7, Pallas kernels: none -> 51.2 us  [the longest x3 19 us: attend(): pl.pallas_call(functools.partial(attend_kernel, 1.0 / math.sqrt(HD)), gri...]
    all_to_all x3 -> x0, waiting for transfers between devices: 45.2 us -> none  [the longest x1 15.8 us: local(): lax.all_to_all(queries.reshape(split_shape), 'fsdp', split_axis=1, concat...]
    ppermute x2 -> x27, starting transfers between devices: 4.31 us -> 38.7 us  [the longest x9 19.9 us: line_move(): return lax.ppermute(value, 'win', pairs)]
    dot_general x8 -> x0, matrix products: 31 us -> none  [the longest x1 13.8 us: local(): jnp.dot(own_heads, full_columns, preferred_element_type=jnp.float32)]
    all_to_all x3 -> x0, starting transfers between devices: 12.1 us -> none  [the longest x1 4.3 us: local(): lax.all_to_all(values.reshape(split_shape), 'fsdp', split_axis=1, concat_...]
    all_gather x1 -> x0, waiting for transfers between devices: 12.1 us -> none  [local(): full_columns = lax.all_gather(out_weight, 'win', axis=1, tiled=True)]
  transfers between devices with their start and end apart: 7 -> 27, of which waited for: 7 -> 11; matrix products, arithmetic and copies ran while one was open for 15% -> 14% of each run, Pallas kernels for 0% -> 21%
where the time goes in v1:
time: 201 us; the launch traced here: 200 us
  waiting for transfers between devices  70.5 us (35%)
  Pallas kernels  51.2 us (25%)
  starting transfers between devices  38.7 us (19%)
  other arithmetic  20 us (10%)
  local copies, waits for them, and re-layouts  17.1 us (9%)
  between operations  2.48 us (1%)
    ppermute x15, waiting for transfers between devices, swap(): return lax.ppermute(value, axis, [(i, i ^ bits) for i in range(size)])  69.1 us
    ppermute x9, starting transfers between devices, line_move(): return lax.ppermute(value, 'win', pairs)  19.9 us
    pallas_call x3, Pallas kernels, attend(): pl.pallas_call(functools.partial(attend_kernel, 1.0 / math.sqrt(HD)), gri...  19 us
    pallas_call x2, Pallas kernels, tally(): pl.pallas_call(functools.partial(tally_kernel, tuple((len(s) for s in sou...  18.2 us
    pallas_call x2, Pallas kernels, give(): pl.pallas_call(functools.partial(give_kernel, tuple((len(s) for s in sour...  14 us
    ppermute x15, starting transfers between devices, swap(): return lax.ppermute(value, axis, [(i, i ^ bits) for i in range(size)])  11.6 us
    unnamed x39, local copies, waits for them, and re-layouts  6.65 us
    another operation x6, other arithmetic, pack(): return jnp.stack([group(v, bits) for v in arrays])  4.91 us
  transfers between devices with their start and end apart: 27, of which 11 were waited for; matrix products, arithmetic and copies ran while one was open for 14% of the time, Pallas kernels for 21%

profile of v1, /device:TPU:0, one launch (start us, length us, event | category | flops | bytes accessed | tf_op | source)
XLA Modules:
  0.0 199.9 jit_solution(16094906660139946100)
XLA Ops:
  0.0 5.9 %collective-permute-start.10 = (bf16[640,640]{1,0:T(8,128)(2,1)}, bf16[640,640]{1,0:T(8,128)(2,1)}, u32[]{:S(2)}, u32[]{:S(2)}) collective-permute-start(bf16[640,640]{1,0:T(8,128)(2,1)} %refs_6_.3), channel_id=1, source_target_pairs={{0,8},{4,12},{8,16},{12,20},{16,24},{20,28},{1,9},{5,13},{9,17},{1... | collective-permute-start | bytes 2457608 | tf_op jit(solution)/shard_map/ppermute | solution.py:25
  7.2 1.6 collective-permute-start.15
  8.7 1.9 dynamic-slice_bitcast_fusion.4
  14.5 1.5 pad_maximum_fusion
  16.8 24.9 %collective-permute-done.2.diag_ref = bf16[2,256,640]{2,1,0:T(8,128)(2,1)} collective-permute-done((bf16[2,256,640]{2,1,0:T(8,128)(2,1)}, bf16[2,256,640]{2,1,0:T(8,128)(2,1)}, u32[]{:S(2)}, u32[]{:S(2)}) %collective-permute-start.2) | collective-permute-done | bytes 655392 | tf_op jit(solution)/shard_map/ppermute | solution.py:20
  43.3 2.4 %dynamic-slice_bitcast_fusion.3 = (bf16[1,256,640]{2,1,0:T(8,128)(2,1)}, bf16[1,256,640]{2,1,0:T(8,128)(2,1)}, bf16[1,256,640]{2,1,0:T(8,128)(2,1)}, bf16[1,256,640]{2,1,0:T(8,128)(2,1)}) fusion(bf16[256,5120]{1,0:T(8,128)(2,1)} %refs_14_.1, s32[]{:T(128)S(6)} %select_n.162, s32[]{:T(128)S(6)} %select_n.165, s32[]{:T(128)S(6)} %select_n.164, s32[]{:T(128)S(6)} %select_n.163), kind=kLoop, calls=%fused_computation.19 | loop fusion | bytes 2621456 | tf_op jit(solution)/shard_map/stack | solution.py:344
  45.7 1.7 collective-permute-start.11
  49.4 5.9 %collective-permute-done.1.far_ref = bf16[2,256,640]{2,1,0:T(8,128)(2,1)} collective-permute-done((bf16[2,256,640]{2,1,0:T(8,128)(2,1)}, bf16[2,256,640]{2,1,0:T(8,128)(2,1)}, u32[]{:S(2)}, u32[]{:S(2)}) %collective-permute-start.1) | collective-permute-done | bytes 655392 | tf_op jit(solution)/shard_map/ppermute | solution.py:20
  55.3 1.5 collective-permute-start.3
  58.9 2.6 %pad_maximum_fusion.1 = bf16[4,256,640]{2,1,0:T(8,128)(2,1)} fusion(bf16[1,256,640]{2,1,0:T(8,128)(2,1)} %get-tuple-element.27, bf16[1,256,640]{2,1,0:T(8,128)(2,1)} %get-tuple-element.28, bf16[1,256,640]{2,1,0:T(8,128)(2,1)} %get-tuple-element.29, bf16[1,256,640]{2,1,0:T(8,128)(2,1)} %get-tuple-element.26), kind=kLoop, calls=%fused_computation.4 | loop fusion | flops 1966080 | bytes 2621440 | tf_op jit(solution)/shard_map/stack | solution.py:344
  61.6 6.1 %collective-permute-done.3.far_ref = bf16[2,256,384]{2,1,0:T(8,128)(2,1)} collective-permute-done((bf16[2,256,384]{2,1,0:T(8,128)(2,1)}, bf16[2,256,384]{2,1,0:T(8,128)(2,1)}, u32[]{:S(2)}, u32[]{:S(2)}) %collective-permute-start.3) | collective-permute-done | bytes 393248 | tf_op jit(solution)/shard_map/ppermute | solution.py:20
  67.6 4.3 %collective-permute-start.16 = (bf16[640,640]{1,0:T(8,128)(2,1)}, bf16[640,640]{1,0:T(8,128)(2,1)S(1)}, u32[]{:S(2)}, u32[]{:S(2)}) collective-permute-start(bf16[640,640]{1,0:T(8,128)(2,1)} %collective-permute-done.15.refs_7_), channel_id=1, source_target_pairs={{0,8},{4,12},{8,16},{12,20},{16,24},{20,28},{1,9},{5,13},{9,17},{1... | collective-permute-start | bytes 2457608 | tf_op jit(solution)/shard_map/ppermute | solution.py:25
  74.9 2.1 %broadcast_select_fusion.refs_6_ = bf16[640,640]{1,0:T(8,128)(2,1)} fusion(bf16[640,640]{1,0:T(8,128)(2,1)} %collective-permute-done.11, bf16[640,640]{1,0:T(8,128)(2,1)} %collective-permute-done.13, pred[]{:T(512)S(6)} %ge.16), kind=kLoop, calls=%fused_computation.7 | loop fusion | flops 409600 | bytes 2457601 | tf_op jit(solution)/shard_map/jit(_where)/select_n | solution.py:349
  79.0 4.2 %collective-permute-done.5.far_ref = bf16[2,256,256]{2,1,0:T(8,128)(2,1)S(1)} collective-permute-done((bf16[2,256,256]{2,1,0:T(8,128)(2,1)S(1)}, bf16[2,256,256]{2,1,0:T(8,128)(2,1)S(1)}, u32[]{:S(2)}, u32[]{:S(2)}) %collective-permute-start.5) | collective-permute-done | bytes 262176 | tf_op jit(solution)/shard_map/ppermute | solution.py:20
  84.5 7.1 %collective-permute-done.6.diag_ref = bf16[2,256,256]{2,1,0:T(8,128)(2,1)S(1)} collective-permute-done((bf16[2,256,256]{2,1,0:T(8,128)(2,1)S(1)}, bf16[2,256,256]{2,1,0:T(8,128)(2,1)S(1)}, u32[]{:S(2)}, u32[]{:S(2)}) %collective-permute-start.6) | collective-permute-done | bytes 262176 | tf_op jit(solution)/shard_map/ppermute | solution.py:20
  93.6 4.8 %shard_map.129.refs_2_ = bf16[2,256,256]{2,1,0:T(8,128)(2,1)} custom-call(s32[2]{0:T(128)} %pad_add_fusion.ids, bf16[256,2560]{1,0:T(8,128)(2,1)} %q_ref.5, bf16[256,2560]{1,0:T(8,128)(2,1)} %k_ref.5, bf16[256,2560]{1,0:T(8,128)(2,1)} %v_ref.5, bf16[2,3,256,640]{3,2,1,0:T(8,128)(2,1)} %copy-done, bf16[2,256,256]{2,1,0:T(8,128)(2,1)} %copy-done.12, ...), custom_call_target="tpu_custom_call" | custom-call | flops 536870912 | bytes 1572864 | tf_op jit(solution)/shard_map/pallas_call | solution.py:54
  99.9 8.3 %shard_map.127.refs_0_ = bf16[2,256,640]{2,1,0:T(8,128)(2,1)} custom-call(s32[2]{0:T(128)} %pad_add_fusion.ids, bf16[256,2560]{1,0:T(8,128)(2,1)} %q_ref.5, bf16[256,2560]{1,0:T(8,128)(2,1)} %k_ref.5, bf16[256,2560]{1,0:T(8,128)(2,1)} %v_ref.5, bf16[2,3,256,640]{3,2,1,0:T(8,128)(2,1)} %copy-done, bf16[2,256,640]{2,1,0:T(8,128)(2,1)} %collective-permute-done.1.far_ref, ...), custom_call_target="tpu_custom_call" | custom-call | flops 1342177280 | bytes 3932160 | tf_op jit(solution)/shard_map/pallas_call | solution.py:54
  108.8 5.9 %shard_map.128.refs_1_ = bf16[2,256,384]{2,1,0:T(8,128)(2,1)} custom-call(s32[2]{0:T(128)} %pad_add_fusion.ids, bf16[256,2560]{1,0:T(8,128)(2,1)} %q_ref.5, bf16[256,2560]{1,0:T(8,128)(2,1)} %k_ref.5, bf16[256,2560]{1,0:T(8,128)(2,1)} %v_ref.5, bf16[2,3,256,640]{3,2,1,0:T(8,128)(2,1)} %copy-done, bf16[2,256,384]{2,1,0:T(8,128)(2,1)} %collective-permute-done.3.far_ref, ...), custom_call_target="tpu_custom_call" | custom-call | flops 805306368 | bytes 2359296 | tf_op jit(solution)/shard_map/pallas_call | solution.py:54
  116.1 1.6 collective-permute-start.19
  117.7 2.1 %collective-permute-start.20 = (bf16[640,640]{1,0:T(8,128)(2,1)}, bf16[640,640]{1,0:T(8,128)(2,1)}, u32[]{:S(2)}, u32[]{:S(2)}) collective-permute-start(bf16[640,640]{1,0:T(8,128)(2,1)} %collective-permute-done.14.refs_10_), channel_id=1, source_target_pairs={{0,2},{1,3},{2,0},{3,1},{4,6},{5,7},{6,4},{7,5},{24,26},{25,27},{2... | collective-permute-start | bytes 2457608 | tf_op jit(solution)/shard_map/ppermute | solution.py:371
  119.9 1.6 collective-permute-start.8
  124.9 8.8 %collective-permute-done.8.refs_4_ = bf16[2,256,384]{2,1,0:T(8,128)(2,1)S(1)} collective-permute-done((bf16[2,256,384]{2,1,0:T(8,128)(2,1)}, bf16[2,256,384]{2,1,0:T(8,128)(2,1)S(1)}, u32[]{:S(2)}, u32[]{:S(2)}) %collective-permute-start.8) | collective-permute-done | bytes 393248 | tf_op jit(solution)/shard_map/ppermute | solution.py:20
  135.3 7.0 %shard_map.131 = bf16[2,2,256,640]{3,2,1,0:T(8,128)(2,1)} custom-call(s32[8]{0:T(128)} %stack.183.ids, bf16[2,256,640]{2,1,0:T(8,128)(2,1)} %shard_map.127.refs_0_, bf16[2,256,384]{2,1,0:T(8,128)(2,1)} %shard_map.128.refs_1_, bf16[2,256,256]{2,1,0:T(8,128)(2,1)} %shard_map.129.refs_2_, bf16[2,256,640]{2,1,0:T(8,128)(2,1)} %copy-done.3, ...), custom_call_target="tpu_custom_call" | custom-call | flops 1677721600 | bytes 4587520 | tf_op jit(solution)/shard_map/pallas_call | solution.py:127
  142.4 7.0 %shard_map.130 = bf16[2,2,256,640]{3,2,1,0:T(8,128)(2,1)} custom-call(s32[8]{0:T(128)} %stack.149.ids, bf16[2,256,640]{2,1,0:T(8,128)(2,1)} %shard_map.127.refs_0_, bf16[2,256,384]{2,1,0:T(8,128)(2,1)} %shard_map.128.refs_1_, bf16[2,256,256]{2,1,0:T(8,128)(2,1)} %shard_map.129.refs_2_, bf16[2,256,640]{2,1,0:T(8,128)(2,1)} %copy-done.3, ...), custom_call_target="tpu_custom_call" | custom-call | flops 1677721600 | bytes 4587520 | tf_op jit(solution)/shard_map/pallas_call | solution.py:127
  149.9 2.3 %copy.28 = bf16[5120,64]{1,0:T(8,128)(2,1)} copy(bf16[5120,64]{0,1:T(8,128)(2,1)} %param.21) | data formatting | bytes 1310720 | tf_op args[8]
  152.3 2.2 %reshape.61 = f32[4,2,640,64]{2,1,0,3:T(2,128)} reshape(f32[5120,64]{0,1:T(8,128)S(1)} %copy-done.6) | data formatting | bytes 2621440 | tf_op jit(solution)/shard_map/reshape | solution.py:410
  155.1 1.7 reduce_sum.47
  157.2 6.8 %collective-permute-done.22.refs_14_.refs_15_ = bf16[4,256,640]{2,1,0:T(8,128)(2,1)S(1)} collective-permute-done((bf16[4,256,640]{2,1,0:T(8,128)(2,1)}, bf16[4,256,640]{2,1,0:T(8,128)(2,1)S(1)}, u32[]{:S(2)}, u32[]{:S(2)}) %collective-permute-start.22) | collective-permute-done | bytes 1310752 | tf_op jit(solution)/shard_map/ppermute | solution.py:20
  165.1 9.0 %shard_map.132.refs_19_ = f32[512,128]{1,0:T(8,128)} custom-call(s32[8]{0:T(128)} %stack.183.ids, bf16[2,256,640]{2,1,0:T(8,128)(2,1)} %shard_map.127.refs_0_, bf16[2,256,384]{2,1,0:T(8,128)(2,1)} %shard_map.128.refs_1_, bf16[2,256,256]{2,1,0:T(8,128)(2,1)} %shard_map.129.refs_2_, bf16[2,256,640]{2,1,0:T(8,128)(2,1)} %copy-done.3, ...), custom_call_target="tpu_custom_call" | custom-call | flops 1677721600 | bytes 4587520 | tf_op jit(solution)/shard_map/pallas_call | solution.py:204
  174.1 9.2 %shard_map.133 = f32[512,128]{1,0:T(8,128)} custom-call(s32[8]{0:T(128)} %stack.149.ids, bf16[2,256,640]{2,1,0:T(8,128)(2,1)} %shard_map.127.refs_0_, bf16[2,256,384]{2,1,0:T(8,128)(2,1)} %shard_map.128.refs_1_, bf16[2,256,256]{2,1,0:T(8,128)(2,1)} %shard_map.129.refs_2_, bf16[2,256,640]{2,1,0:T(8,128)(2,1)} %copy-done.3, bf16[2,256,384]{2,1,0:T(8,128)(2,1)} %copy-done.4, ...), custom_call_target="tpu_custom_call" | custom-call | flops 1677721600 | bytes 4587520 | tf_op jit(solution)/shard_map/pallas_call | solution.py:204
  184.8 4.4 %collective-permute-done.24 = f32[256,128]{1,0:T(8,128)S(1)} collective-permute-done((f32[256,128]{1,0:T(8,128)S(1)}, f32[256,128]{1,0:T(8,128)S(1)}, u32[]{:S(2)}, u32[]{:S(2)}) %collective-permute-start.24) | collective-permute-done | bytes 131104 | tf_op jit(solution)/shard_map/ppermute | solution.py:20
  193.2 4.5 %collective-permute-start.26 = (bf16[4,1024]{1,0:T(4,128)(2,1)S(1)}, bf16[4,1024]{1,0:T(4,128)(2,1)S(1)}, u32[]{:S(2)}, u32[]{:S(2)}) collective-permute-start(bf16[4,1024]{1,0:T(4,128)(2,1)S(1)} %get-tuple-element.43), channel_id=1, source_target_pairs={{4,0},{8,4},{12,8},{16,12},{20,16},{24,20},{28,24},{0,28},{5,1},{9... | collective-permute-start | bytes 24584 | tf_op jit(solution)/shard_map/ppermute | solution.py:435
  (119 shorter events, 36.4 us)
Async XLA Ops:
  0.0 45.7 %collective-permute-start.10 = (bf16[640,640]{1,0:T(8,128)(2,1)}, bf16[640,640]{1,0:T(8,128)(2,1)}, u32[]{:S(2)}, u32[]{:S(2)}) collective-permute-start(bf16[640,640]{1,0:T(8,128)(2,1)} %refs_6_.3), channel_id=1, source_target_pairs={{0,8},{4,12},{8,16},{12,20},{16,24},{20,28},{1,9},{5,13},{9,17},{1... | collective-permute-start | bytes 2457608 | tf_op jit(solution)/shard_map/ppermute | solution.py:25
  5.9 41.5 %collective-permute-start.12 = (bf16[640,640]{1,0:T(8,128)(2,1)}, bf16[640,640]{1,0:T(8,128)(2,1)}, u32[]{:S(2)}, u32[]{:S(2)}) collective-permute-start(bf16[640,640]{1,0:T(8,128)(2,1)} %refs_6_.3), channel_id=1, source_target_pairs={{8,0},{12,4},{16,8},{20,12},{24,16},{28,20},{9,1},{13,5},{17,9},{2... | collective-permute-start | bytes 2457608 | tf_op jit(solution)/shard_map/ppermute | solution.py:25
  7.2 49.7 %collective-permute-start.15 = (bf16[640,640]{1,0:T(8,128)(2,1)}, bf16[640,640]{1,0:T(8,128)(2,1)}, u32[]{:S(2)}, u32[]{:S(2)}) collective-permute-start(bf16[640,640]{1,0:T(8,128)(2,1)} %refs_6_.3), channel_id=1, source_target_pairs={{0,2},{1,3},{2,0},{3,1},{4,6},{5,7},{6,4},{7,5},{8,10},{9,11},{10,... | collective-permute-start | bytes 2457608 | tf_op jit(solution)/shard_map/ppermute | solution.py:20
  11.6 30.1 %collective-permute-start.2 = (bf16[2,256,640]{2,1,0:T(8,128)(2,1)}, bf16[2,256,640]{2,1,0:T(8,128)(2,1)}, u32[]{:S(2)}, u32[]{:S(2)}) collective-permute-start(bf16[2,256,640]{2,1,0:T(8,128)(2,1)} %pad_maximum_fusion.3), channel_id=1, source_target_pairs={{0,3},{1,2},{2,1},{3,0},{4,7},{5,6},{6,5},{7,4},{8,11},{9,10},{10,... | collective-permute-start | bytes 1966088 | tf_op jit(solution)/shard_map/ppermute | solution.py:20
  12.5 42.8 %collective-permute-start.1 = (bf16[2,256,640]{2,1,0:T(8,128)(2,1)}, bf16[2,256,640]{2,1,0:T(8,128)(2,1)}, u32[]{:S(2)}, u32[]{:S(2)}) collective-permute-start(bf16[2,256,640]{2,1,0:T(8,128)(2,1)} %pad_maximum_fusion.2), channel_id=1, source_target_pairs={{0,2},{1,3},{2,0},{3,1},{4,6},{5,7},{6,4},{7,5},{8,10},{9,11},{10,... | collective-permute-start | bytes 1966088 | tf_op jit(solution)/shard_map/ppermute | solution.py:20
  41.7 49.9 %collective-permute-start = (bf16[2,3,256,640]{3,2,1,0:T(8,128)(2,1)}, bf16[2,3,256,640]{3,2,1,0:T(8,128)(2,1)S(1)}, u32[]{:S(2)}, u32[]{:S(2)}) collective-permute-start(bf16[2,3,256,640]{3,2,1,0:T(8,128)(2,1)} %pad_maximum_fusion), channel_id=1, source_target_pairs={{0,1},{1,0},{2,3},{3,2},{4,5},{5,4},{6,7},{7,6},{8,9},{9,8},{10,11... | collective-permute-start | bytes 5898248 | tf_op jit(solution)/shard_map/ppermute | solution.py:20
  45.7 28.4 %collective-permute-start.11 = (bf16[640,640]{1,0:T(8,128)(2,1)}, bf16[640,640]{1,0:T(8,128)(2,1)}, u32[]{:S(2)}, u32[]{:S(2)}) collective-permute-start(bf16[640,640]{1,0:T(8,128)(2,1)} %collective-permute-done.10.refs_9_), channel_id=1, source_target_pairs={{8,16},{12,20},{16,24},{20,28},{9,17},{13,21},{17,25},{21,29},{10,... | collective-permute-start | bytes 2457608 | tf_op jit(solution)/shard_map/ppermute | solution.py:25
  47.4 27.5 %collective-permute-start.13 = (bf16[640,640]{1,0:T(8,128)(2,1)}, bf16[640,640]{1,0:T(8,128)(2,1)}, u32[]{:S(2)}, u32[]{:S(2)}) collective-permute-start(bf16[640,640]{1,0:T(8,128)(2,1)} %collective-permute-done.12.refs_8_), channel_id=1, source_target_pairs={{8,0},{12,4},{16,8},{20,12},{9,1},{13,5},{17,9},{21,13},{10,2},{14... | collective-permute-start | bytes 2457608 | tf_op jit(solution)/shard_map/ppermute | solution.py:25
  55.3 12.3 %collective-permute-start.3 = (bf16[2,256,384]{2,1,0:T(8,128)(2,1)}, bf16[2,256,384]{2,1,0:T(8,128)(2,1)}, u32[]{:S(2)}, u32[]{:S(2)}) collective-permute-start(bf16[2,256,384]{2,1,0:T(8,128)(2,1)} %fusion.2), channel_id=1, source_target_pairs={{0,2},{1,3},{2,0},{3,1},{4,6},{5,7},{6,4},{7,5},{8,10},{9,11},{10,... | collective-permute-start | bytes 1179656 | tf_op jit(solution)/shard_map/ppermute | solution.py:20
  56.8 16.0 %collective-permute-start.4 = (bf16[2,256,384]{2,1,0:T(8,128)(2,1)}, bf16[2,256,384]{2,1,0:T(8,128)(2,1)}, u32[]{:S(2)}, u32[]{:S(2)}) collective-permute-start(bf16[2,256,384]{2,1,0:T(8,128)(2,1)} %fusion.1), channel_id=1, source_target_pairs={{0,3},{1,2},{2,1},{3,0},{4,7},{5,6},{6,5},{7,4},{8,11},{9,10},{10,... | collective-permute-start | bytes 1179656 | tf_op jit(solution)/shard_map/ppermute | solution.py:20
  61.6 21.6 %copy-start.9 = (bf16[2,256,256]{2,1,0:T(8,128)(2,1)S(1)}, bf16[2,256,256]{2,1,0:T(8,128)(2,1)}, u32[]{:S(2)}) copy-start(bf16[2,256,256]{2,1,0:T(8,128)(2,1)} %pad_maximum_fusion.4) | copy-start | bytes 786436
  67.6 47.1 %collective-permute-start.16 = (bf16[640,640]{1,0:T(8,128)(2,1)}, bf16[640,640]{1,0:T(8,128)(2,1)S(1)}, u32[]{:S(2)}, u32[]{:S(2)}) collective-permute-start(bf16[640,640]{1,0:T(8,128)(2,1)} %collective-permute-done.15.refs_7_), channel_id=1, source_target_pairs={{0,8},{4,12},{8,16},{12,20},{16,24},{20,28},{1,9},{5,13},{9,17},{1... | collective-permute-start | bytes 2457608 | tf_op jit(solution)/shard_map/ppermute | solution.py:25
  72.8 41.9 %collective-permute-start.17 = (bf16[640,640]{1,0:T(8,128)(2,1)}, bf16[640,640]{1,0:T(8,128)(2,1)}, u32[]{:S(2)}, u32[]{:S(2)}) collective-permute-start(bf16[640,640]{1,0:T(8,128)(2,1)} %collective-permute-done.15.refs_7_), channel_id=1, source_target_pairs={{8,0},{12,4},{16,8},{20,12},{24,16},{28,20},{9,1},{13,5},{17,9},{2... | collective-permute-start | bytes 2457608 | tf_op jit(solution)/shard_map/ppermute | solution.py:25
  74.1 9.1 %collective-permute-start.5 = (bf16[2,256,256]{2,1,0:T(8,128)(2,1)S(1)}, bf16[2,256,256]{2,1,0:T(8,128)(2,1)S(1)}, u32[]{:S(2)}, u32[]{:S(2)}) collective-permute-start(bf16[2,256,256]{2,1,0:T(8,128)(2,1)S(1)} %copy-done.10), channel_id=1, source_target_pairs={{0,2},{1,3},{2,0},{3,1},{4,6},{5,7},{6,4},{7,5},{8,10},{9,11},{10,... | collective-permute-start | bytes 786440 | tf_op jit(solution)/shard_map/ppermute | solution.py:20
  77.0 37.8 %collective-permute-start.14 = (bf16[640,640]{1,0:T(8,128)(2,1)}, bf16[640,640]{1,0:T(8,128)(2,1)}, u32[]{:S(2)}, u32[]{:S(2)}) collective-permute-start(bf16[640,640]{1,0:T(8,128)(2,1)} %broadcast_select_fusion.refs_6_), channel_id=1, source_target_pairs={{16,24},{20,28},{8,0},{12,4},{17,25},{21,29},{9,1},{13,5},{18,26},... | collective-permute-start | bytes 2457608 | tf_op jit(solution)/shard_map/ppermute | solution.py:25
  83.2 8.4 %collective-permute-start.6 = (bf16[2,256,256]{2,1,0:T(8,128)(2,1)S(1)}, bf16[2,256,256]{2,1,0:T(8,128)(2,1)S(1)}, u32[]{:S(2)}, u32[]{:S(2)}) collective-permute-start(bf16[2,256,256]{2,1,0:T(8,128)(2,1)S(1)} %copy-done.9), channel_id=1, source_target_pairs={{0,3},{1,2},{2,1},{3,0},{4,7},{5,6},{6,5},{7,4},{8,11},{9,10},{10,... | collective-permute-start | bytes 786440 | tf_op jit(solution)/shard_map/ppermute | solution.py:20
  98.4 21.5 %collective-permute-start.9 = (bf16[2,256,256]{2,1,0:T(8,128)(2,1)}, bf16[2,256,256]{2,1,0:T(8,128)(2,1)S(1)}, u32[]{:S(2)}, u32[]{:S(2)}) collective-permute-start(bf16[2,256,256]{2,1,0:T(8,128)(2,1)} %shard_map.129.refs_2_), channel_id=1, source_target_pairs={{0,4},{4,0},{8,12},{12,8},{16,20},{20,16},{24,28},{28,24},{1,5},{5... | collective-permute-start | bytes 786440 | tf_op jit(solution)/shard_map/ppermute | solution.py:20
  108.2 15.3 %copy-start.8 = (bf16[5120,64]{0,1:T(8,128)(2,1)S(1)}, bf16[5120,64]{0,1:T(8,128)(2,1)}, u32[]{:S(2)}) copy-start(bf16[5120,64]{0,1:T(8,128)(2,1)} %param.21) | copy-start | bytes 1966084
  108.2 15.3 %copy-start.14 = (f32[5120]{0:T(1024)S(1)}, f32[5120]{0:T(1024)}, u32[]{:S(2)}) copy-start(f32[5120]{0:T(1024)} %param.20) | copy-start | bytes 61444
  108.2 15.3 %copy-start.15 = (f32[5120]{0:T(1024)S(1)}, f32[5120]{0:T(1024)}, u32[]{:S(2)}) copy-start(f32[5120]{0:T(1024)} %param.19) | copy-start | bytes 61444
  108.2 26.0 %collective-permute-start.7 = (bf16[2,256,640]{2,1,0:T(8,128)(2,1)}, bf16[2,256,640]{2,1,0:T(8,128)(2,1)S(1)}, u32[]{:S(2)}, u32[]{:S(2)}) collective-permute-start(bf16[2,256,640]{2,1,0:T(8,128)(2,1)} %shard_map.127.refs_0_), channel_id=1, source_target_pairs={{0,4},{4,0},{8,12},{12,8},{16,20},{20,16},{24,28},{28,24},{1,5},{5... | collective-permute-start | bytes 1966088 | tf_op jit(solution)/shard_map/ppermute | solution.py:20
  114.8 19.5 %copy-start.2 = (bf16[640,640]{1,0:T(8,128)(2,1)}, bf16[640,640]{1,0:T(8,128)(2,1)S(1)}, u32[]{:S(2)}) copy-start(bf16[640,640]{1,0:T(8,128)(2,1)S(1)} %collective-permute-done.16.refs_11_) | copy-start | bytes 2457604
  114.8 27.6 %collective-permute-start.18 = (bf16[640,640]{1,0:T(8,128)(2,1)}, bf16[640,640]{1,0:T(8,128)(2,1)}, u32[]{:S(2)}, u32[]{:S(2)}) collective-permute-start(bf16[640,640]{1,0:T(8,128)(2,1)} %collective-permute-done.17.refs_10_), channel_id=1, source_target_pairs={{8,0},{12,4},{16,8},{20,12},{9,1},{13,5},{17,9},{21,13},{10,2},{14... | collective-permute-start | bytes 2457608 | tf_op jit(solution)/shard_map/ppermute | solution.py:25
  116.1 26.3 %collective-permute-start.19 = (bf16[640,640]{1,0:T(8,128)(2,1)S(1)}, bf16[640,640]{1,0:T(8,128)(2,1)}, u32[]{:S(2)}, u32[]{:S(2)}) collective-permute-start(bf16[640,640]{1,0:T(8,128)(2,1)S(1)} %collective-permute-done.16.refs_11_), channel_id=1, source_target_pairs={{8,16},{12,20},{16,24},{20,28},{9,17},{13,21},{17,25},{21,29},{10,... | collective-permute-start | bytes 2457608 | tf_op jit(solution)/shard_map/ppermute | solution.py:25
  117.7 24.7 %collective-permute-start.20 = (bf16[640,640]{1,0:T(8,128)(2,1)}, bf16[640,640]{1,0:T(8,128)(2,1)}, u32[]{:S(2)}, u32[]{:S(2)}) collective-permute-start(bf16[640,640]{1,0:T(8,128)(2,1)} %collective-permute-done.14.refs_10_), channel_id=1, source_target_pairs={{0,2},{1,3},{2,0},{3,1},{4,6},{5,7},{6,4},{7,5},{24,26},{25,27},{2... | collective-permute-start | bytes 2457608 | tf_op jit(solution)/shard_map/ppermute | solution.py:371
  119.9 13.8 %collective-permute-start.8 = (bf16[2,256,384]{2,1,0:T(8,128)(2,1)}, bf16[2,256,384]{2,1,0:T(8,128)(2,1)S(1)}, u32[]{:S(2)}, u32[]{:S(2)}) collective-permute-start(bf16[2,256,384]{2,1,0:T(8,128)(2,1)} %shard_map.128.refs_1_), channel_id=1, source_target_pairs={{0,4},{4,0},{8,12},{12,8},{16,20},{20,16},{24,28},{28,24},{1,5},{5... | collective-permute-start | bytes 1179656 | tf_op jit(solution)/shard_map/ppermute | solution.py:20
  133.7 30.3 %collective-permute-start.22 = (bf16[4,256,640]{2,1,0:T(8,128)(2,1)}, bf16[4,256,640]{2,1,0:T(8,128)(2,1)S(1)}, u32[]{:S(2)}, u32[]{:S(2)}) collective-permute-start(bf16[4,256,640]{2,1,0:T(8,128)(2,1)} %pad_maximum_fusion.1), channel_id=1, source_target_pairs={{0,4},{4,0},{8,12},{12,8},{16,20},{20,16},{24,28},{28,24},{1,5},{5... | collective-permute-start | bytes 3932168 | tf_op jit(solution)/shard_map/ppermute | solution.py:20
  142.3 21.7 %collective-permute-start.23 = (bf16[2,2,256,640]{3,2,1,0:T(8,128)(2,1)}, bf16[2,2,256,640]{3,2,1,0:T(8,128)(2,1)}, u32[]{:S(2)}, u32[]{:S(2)}) collective-permute-start(bf16[2,2,256,640]{3,2,1,0:T(8,128)(2,1)} %shard_map.131), channel_id=1, source_target_pairs={{0,1},{1,0},{2,3},{3,2},{4,5},{5,4},{6,7},{7,6},{8,9},{9,8},{10,11... | collective-permute-start | bytes 3932168 | tf_op jit(solution)/shard_map/ppermute | solution.py:20
  149.4 24.7 %collective-permute-start.21 = (bf16[2,2,256,640]{3,2,1,0:T(8,128)(2,1)}, bf16[2,2,256,640]{3,2,1,0:T(8,128)(2,1)}, u32[]{:S(2)}, u32[]{:S(2)}) collective-permute-start(bf16[2,2,256,640]{3,2,1,0:T(8,128)(2,1)} %shard_map.130), channel_id=1, source_target_pairs={{0,1},{1,0},{2,3},{3,2},{4,5},{5,4},{6,7},{7,6},{8,9},{9,8},{10,11... | collective-permute-start | bytes 3932168 | tf_op jit(solution)/shard_map/ppermute | solution.py:20
  184.2 5.0 %collective-permute-start.24 = (f32[256,128]{1,0:T(8,128)S(1)}, f32[256,128]{1,0:T(8,128)S(1)}, u32[]{:S(2)}, u32[]{:S(2)}) collective-permute-start(f32[256,128]{1,0:T(8,128)S(1)} %slice.166), channel_id=1, source_target_pairs={{0,4},{4,0},{8,12},{12,8},{16,20},{20,16},{24,28},{28,24},{1,5},{5... | collective-permute-start | bytes 393224 | tf_op jit(solution)/shard_map/ppermute | solution.py:20
  192.0 6.7 %collective-permute-start.25 = (bf16[4,1024]{1,0:T(4,128)(2,1)S(1)}, bf16[4,1024]{1,0:T(4,128)(2,1)S(1)}, u32[]{:S(2)}, u32[]{:S(2)}) collective-permute-start(bf16[4,1024]{1,0:T(4,128)(2,1)S(1)} %get-tuple-element.42), channel_id=1, source_target_pairs={{0,4},{4,8},{8,12},{12,16},{16,20},{20,24},{24,28},{28,0},{1,5},{5... | collective-permute-start | bytes 24584 | tf_op jit(solution)/shard_map/ppermute | solution.py:434
  193.2 5.9 %collective-permute-start.26 = (bf16[4,1024]{1,0:T(4,128)(2,1)S(1)}, bf16[4,1024]{1,0:T(4,128)(2,1)S(1)}, u32[]{:S(2)}, u32[]{:S(2)}) collective-permute-start(bf16[4,1024]{1,0:T(4,128)(2,1)S(1)} %get-tuple-element.43), channel_id=1, source_target_pairs={{4,0},{8,4},{12,8},{16,12},{20,16},{24,20},{28,24},{0,28},{5,1},{9... | collective-permute-start | bytes 24584 | tf_op jit(solution)/shard_map/ppermute | solution.py:435
  (13 other events, 69.7 us)

commit v2 on v1

v2 whole, which is shorter than its diff:
```python
import functools
import math

import jax
import jax.numpy as jnp
from jax import lax
from jax.experimental import pallas as pl
from jax.experimental.pallas import tpu as pltpu
from jax.sharding import PartitionSpec as P


HD = 128
FD = 4
EPSILON = 0.001
LANES = 128


WHOLE = pltpu.CompilerParams(vmem_limit_bytes=67043328)


def swap(value, axis, bits):
    size = lax.axis_size(axis)
    return lax.ppermute(value, axis, [(i, i ^ bits) for i in range(size)])


def line_move(value, moves):
    pairs = [(2 * a + p, 2 * b + p) for a, b in moves for p in range(2)]
    return lax.ppermute(value, "win", pairs)


def attend_kernel(score_scale, ids, q_ref, k_ref, v_ref, mate_ref, far_ref, diag_ref, out_ref):
    keys = [k_ref[...], mate_ref[0, 1], far_ref[0], diag_ref[0]]
    values = [v_ref[...], mate_ref[0, 2], far_ref[1], diag_ref[1]]
    factor = score_scale * math.log2(math.e)
    for half, query in enumerate((q_ref[...], mate_ref[0, 0])):
        scores = [
            lax.dot_general(query, k, (((1,), (1,)), ((), ())), preferred_element_type=jnp.float32)
            for k in keys
        ]
        peaks = [jnp.max(s, axis=-1, keepdims=True) for s in scores]
        highest = functools.reduce(jnp.maximum, peaks)
        total = None
        summed = None
        for s, v in zip(scores, values):
            exponent = jnp.exp2((s - highest) * factor)
            part = jnp.sum(exponent, axis=-1, keepdims=True)
            prod = jnp.dot(exponent.astype(jnp.bfloat16), v, preferred_element_type=jnp.float32)
            total = part if total is None else total + part
            summed = prod if summed is None else summed + prod
        out_ref[half] = (summed / total).astype(jnp.bfloat16)


def attend(ids, queries, keys, values, mate, far, diag, part, first, count, heads):
    rows = queries.shape[0]
    wide = pl.BlockSpec((rows, HD), lambda h, ids: (0, ids[part] * heads + first + h))
    narrow = pl.BlockSpec((2, rows, HD), lambda h, ids: (0, 0, h))
    return pl.pallas_call(
        functools.partial(attend_kernel, 1.0 / math.sqrt(HD)),
        grid_spec=pltpu.PrefetchScalarGridSpec(
            num_scalar_prefetch=1,
            grid=(count,),
            in_specs=[wide] * 3
            + [pl.BlockSpec((1, 3, rows, HD), lambda h, ids: (part, 0, 0, first + h))]
            + [narrow] * 2,
            out_specs=narrow,
        ),
        out_shape=jax.ShapeDtypeStruct((2, rows, count * HD), jnp.bfloat16),
        compiler_params=WHOLE,
        cost_estimate=pl.CostEstimate(
            flops=32 * rows * rows * HD * count,
            bytes_accessed=24 * rows * HD * count,
            transcendentals=8 * rows * rows * count,
        ),
    )(ids, queries, keys, values, mate, far, diag)


class Fetch:
    def __init__(self, sems):
        self.sems = sems
        self.count = 0

    def start(self, source, target):
        copy = pltpu.make_async_copy(source, target, self.sems.at[self.count])
        self.count += 1
        copy.start()
        return copy

    def start_one_of(self, index, sources, target):
        copies = [pltpu.make_async_copy(v, target, self.sems.at[self.count]) for v in sources]
        self.count += 1
        for c, copy in enumerate(copies):
            if len(copies) == 1:
                copy.start()
            else:
                pl.when(index == c)(copy.start)
        return copies[0]


def project_kernel(halves, picks, chunks, added, ids, *refs):
    blocks = len(picks)
    att = refs[: 2 * chunks]
    at = 2 * chunks + sum(sum(p) for p in picks)
    sources = list(refs[2 * chunks : at])
    part_ref = refs[at] if added else None
    out_ref, side, held, made, before, sems, out_sems = refs[at + added :]
    rows = side.shape[2]
    depth = held.shape[1] // len(picks[0])
    fetch = Fetch(sems)
    coming = []
    for w in range(2):
        start = 0
        for part in att[w * chunks : (w + 1) * chunks]:
            cols = part.shape[-1]
            source = part if len(halves) == 2 else part.at[pl.ds(halves[0], 1)]
            coming.append(fetch.start(source, side.at[:, w, :, pl.ds(start, cols)]))
            start += cols

    def weights(b):
        waits = []
        for j, pick in enumerate(picks[b]):
            options = [sources.pop(0) for _ in range(pick)]
            place = held.at[b, pl.ds(j * depth, depth), :]
            waits.append(fetch.start_one_of(ids[len(picks[0]) * b + j], options, place))
        if added:
            waits.append(fetch.start(part_ref.at[b, halves[0]], before.at[b]))
        return waits

    queue = [coming + weights(0)] + [weights(b) for b in range(1, min(blocks, 2))]
    leaving = []
    for b in range(blocks):
        for copy in queue[b]:
            copy.wait()
        if b + 2 < blocks:
            queue.append(weights(b + 2))
        for h in range(len(halves)):
            both = side[h].reshape(2 * rows, side.shape[3])
            part = jnp.dot(both, held[b], preferred_element_type=jnp.float32)
            for w in range(2):
                piece = part[w * rows : (w + 1) * rows]
                if added:
                    piece = piece + before[b, w].astype(jnp.float32)
                made[b, h, w] = piece.astype(jnp.bfloat16)
            copy = pltpu.make_async_copy(made.at[b, h], out_ref.at[b, h], out_sems.at[b, h])
            copy.start()
            leaving.append(copy)
    for copy in leaving:
        copy.wait()


def project(ids, halves, att, sources, added=None):
    rows = att[0].shape[1]
    depth, span = sources[0][0][0].shape
    blocks = len(sources)
    picks = tuple(tuple(len(o) for o in block) for block in sources)
    width = depth * len(picks[0])
    flat = [v for block in sources for options in block for v in options]
    shape = (blocks, len(halves), 2, rows, span)
    extra = [] if added is None else [added]
    hbm = pl.BlockSpec(memory_space=pltpu.HBM)
    return pl.pallas_call(
        functools.partial(project_kernel, halves, picks, len(att) // 2, len(extra)),
        in_specs=[pl.BlockSpec(memory_space=pltpu.SMEM)]
        + [hbm] * (len(att) + len(flat) + len(extra)),
        out_specs=hbm,
        scratch_shapes=[
            pltpu.VMEM((len(halves), 2, rows, width), jnp.bfloat16),
            pltpu.VMEM((blocks, width, span), jnp.bfloat16),
            pltpu.VMEM(shape, jnp.bfloat16),
            pltpu.VMEM((blocks if extra else 1, 2, rows, span), jnp.bfloat16),
            pltpu.SemaphoreType.DMA((len(att) + blocks * (len(picks[0]) + 1),)),
            pltpu.SemaphoreType.DMA((blocks, len(halves))),
        ],
        out_shape=jax.ShapeDtypeStruct(shape, jnp.bfloat16),
        compiler_params=WHOLE,
        cost_estimate=pl.CostEstimate(
            flops=4 * rows * len(halves) * width * span * blocks,
            bytes_accessed=8 * rows * width + 2 * blocks * width * span,
            transcendentals=0,
        ),
    )(ids, *att, *flat, *extra)


def tally_kernel(first, last, ids, keep_ref, got_ref, own_ref, other_ref, gate_ref, scale_ref, head_ref, *refs):
    state_ref = None if first else refs[0]
    out_refs = refs[(not first) : -6]
    keep, got, own, other, head, sems = refs[-6:]
    blocks, _, rows, span = keep.shape
    chans = head_ref.shape[2]
    fetch = Fetch(sems)
    place = [ids[b] for b in range(blocks)]
    coming = []
    for b in range(blocks):
        column = pl.ds(pl.multiple_of(place[b] * span, LANES), span)
        coming.append(
            [
                fetch.start(keep_ref.at[b, 0], keep.at[b]),
                fetch.start(got_ref.at[b, 0], got.at[b]),
                fetch.start(own_ref.at[:, column], own.at[b]),
                fetch.start(other_ref.at[ids[blocks + b]], other.at[b]),
                fetch.start(head_ref.at[place[b]], head.at[b]),
            ]
        )
    state = [None] * 2
    if not first:
        for w in range(2):
            old = state_ref[w]
            parts = [old[:, chans + i : chans + i + 1] for i in range(3)]
            state[w] = tuple(parts) + (old[:, :chans],)
    for b in range(blocks):
        for copy in coming[b]:
            copy.wait()
        gate = gate_ref[place[b]]
        scale = scale_ref[place[b]]
        for w, stream in enumerate((own, other)):
            proj = keep[b, w].astype(jnp.float32) + got[b, w].astype(jnp.float32)
            hidden = stream[b].astype(jnp.float32) + gate * proj
            if state[w] is None:
                centre = jnp.mean(hidden, axis=-1, keepdims=True)
            else:
                centre = state[w][0]
            moved = hidden - centre
            dots = jnp.dot(
                (moved * scale).astype(jnp.bfloat16), head[b], preferred_element_type=jnp.float32
            )
            one = jnp.sum(moved, axis=-1, keepdims=True)
            two = jnp.sum(moved * moved, axis=-1, keepdims=True)
            if state[w] is not None:
                one, two, dots = one + state[w][1], two + state[w][2], dots + state[w][3]
            state[w] = (centre, one, two, dots)
    sums_ref = out_refs[0]
    for w, (centre, one, two, dots) in enumerate(state):
        sums_ref[w, :, :chans] = dots
        lane = lax.broadcasted_iota(jnp.int32, (rows, sums_ref.shape[2] - chans), 1)
        sums_ref[w, :, chans:] = jnp.where(
            lane == 0, centre, jnp.where(lane == 1, one, jnp.where(lane == 2, two, 0.0))
        )
    if last:
        across_ref, ahead_ref, behind_ref, beside_ref = out_refs[1:]
        edge = ahead_ref.shape[0]
        odd = ids[2 * blocks]
        inner = pl.ds(pl.multiple_of((1 - odd) * (rows - edge), 8), edge)
        outer = pl.ds(pl.multiple_of(odd * (rows - edge), 8), edge)
        across_ref[:rows] = sums_ref[1]
        across_ref[rows:] = sums_ref[0, inner]
        ahead_ref[...] = sums_ref[1, inner]
        behind_ref[...] = sums_ref[0, outer]
        beside_ref[...] = sums_ref[1, outer]


def tally(ids, keep, got, own, other, gate, scale, head, state, edge):
    blocks, _, _, rows, span = keep.shape
    chans = head.shape[2]
    lanes = chans + LANES - chans % LANES
    old = [] if state is None else [state]
    anywhere = pl.BlockSpec(memory_space=pltpu.HBM)
    near_by = pl.BlockSpec(memory_space=pltpu.VMEM)
    shapes = [(2, rows, lanes)]
    if edge:
        shapes += [(rows + edge, lanes)] + [(edge, lanes)] * 3
    return pl.pallas_call(
        functools.partial(tally_kernel, state is None, edge > 0),
        in_specs=[pl.BlockSpec(memory_space=pltpu.SMEM)]
        + [anywhere] * 4
        + [near_by] * 2
        + [anywhere]
        + [near_by] * len(old),
        out_specs=[near_by] * len(shapes),
        scratch_shapes=[
            pltpu.VMEM((blocks, 2, rows, span), jnp.bfloat16),
            pltpu.VMEM((blocks, 2, rows, span), jnp.bfloat16),
            pltpu.VMEM((blocks, rows, span), jnp.bfloat16),
            pltpu.VMEM((blocks, rows, span), jnp.bfloat16),
            pltpu.VMEM((blocks, span, chans), jnp.bfloat16),
            pltpu.SemaphoreType.DMA((5 * blocks,)),
        ],
        out_shape=[jax.ShapeDtypeStruct(s, jnp.float32) for s in shapes],
        compiler_params=WHOLE,
        cost_estimate=pl.CostEstimate(
            flops=4 * rows * span * blocks * (chans + 8),
            bytes_accessed=12 * rows * span * blocks,
            transcendentals=0,
        ),
    )(ids, keep, got, own, other, gate, scale, head, *old)


def terms_kernel(split, odd_ref, scale_ref, shift_ref, head_ref, out_ref):
    sums = [0.0, 0.0]
    offset = 0.0
    exact = functools.partial(
        jnp.dot, precision=lax.Precision.HIGHEST, preferred_element_type=jnp.float32
    )
    for b in range(head_ref.shape[0]):
        head = head_ref[b].astype(jnp.float32)
        both = exact(jnp.concatenate([scale_ref[b], shift_ref[b]] * 4), head)
        half = b // split % 2
        sums[half] = sums[half] + both[0:1]
        offset = offset + both[1:2]
    odd = odd_ref[0] == 1
    out_ref[0:1] = jnp.where(odd, sums[1], sums[0])
    out_ref[1:2] = jnp.where(odd, sums[0], sums[1])
    out_ref[2:3] = offset


def finish_kernel(
    model, ids, step_ref, shares_ref, ramps_ref, mine_ref, beside_ref, ahead_ref, got_ref,
    behind_ref, terms_ref, latents_ref, tail_ref, start_ref, out_ref, speed, outer
):
    rows, chans = speed.shape
    frames = latents_ref.shape[0]
    per_frame = rows // frames
    own_cw, their_cw, offset = (terms_ref[i : i + 1] for i in range(3))

    def combine(a, b):
        mid_a, one_a, two_a = (a[:, chans + i : chans + i + 1] for i in range(3))
        mid_b, one_b, two_b = (b[:, chans + i : chans + i + 1] for i in range(3))
        centre = (one_a + one_b) / model + 0.5 * (mid_a + mid_b)
        da = centre - mid_a
        db = centre - mid_b
        half = model // 2
        square = (two_a - 2.0 * da * one_a + half * da * da) + (
            two_b - 2.0 * db * one_b + half * db * db
        )
        inverse = 1.0 / jnp.sqrt(square / model + EPSILON)
        dots = a[:, :chans] + b[:, :chans] - da * own_cw - db * their_cw
        return dots * inverse + offset

    speed[...] = combine(mine_ref[0], got_ref[:rows])
    beside = combine(beside_ref[...], got_ref[rows:])
    outside = combine(ahead_ref[...], behind_ref[...])
    odd = ids[0] == 1
    outer[0] = jnp.where(odd, beside, outside)
    outer[1] = jnp.where(odd, outside, beside)
    step = step_ref[0]
    window = ids[1]
    previous = ids[2]
    over_prev = shares_ref[previous]
    over_next = shares_ref[window]
    frame = lax.broadcasted_iota(jnp.int32, (frames, 1), 0)
    column = lambda scalar: jnp.full((frames, 1), scalar, jnp.int32).astype(jnp.float32)
    zero = jnp.zeros((frames, 1), jnp.float32)
    takes = []
    mine = zero
    theirs = zero
    for j in range(FD):
        at = j - FD + over_prev
        pick = (frame == at) & (frame < over_prev)
        near = jnp.maximum(at, 0)
        takes.append((0, j, pick))
        theirs = jnp.where(pick, column(ramps_ref[previous, 2 * near]), theirs)
        mine = jnp.where(pick, column(ramps_ref[previous, 2 * near + 1]), mine)
    for j in range(FD):
        pick = (frame == j + frames - over_next) & (frame >= over_prev)
        takes.append((1, j, pick))
        mine = jnp.where(pick, column(ramps_ref[window, 2 * j]), mine)
        theirs = jnp.where(pick, column(ramps_ref[window, 2 * j + 1]), theirs)
    alone = mine + theirs == 0.0
    mine = jnp.where(alone, 1.0, mine)
    total = mine + theirs
    for p in range(per_frame):
        lanes = slice(p * chans, (p + 1) * chans)
        fresh = latents_ref[:, lanes] + step * speed[pl.ds(p, frames, stride=per_frame), :]
        sides = [
            ref[:, lanes] + step * outer[side, pl.ds(p, FD, stride=per_frame), :]
            for side, ref in enumerate((tail_ref, start_ref))
        ]
        other = jnp.zeros_like(fresh)
        for side, j, pick in takes:
            other = jnp.where(pick, sides[side][j : j + 1], other)
        out_ref[:, lanes] = (mine * fresh + theirs * other) / total


def after(*values):
    return lax.optimization_barrier(values)


def local(
    queries,
    keys,
    values,
    stream,
    out_weight,
    gate,
    head_shift,
    head_scale,
    head_weight,
    latents,
    step_size,
    intersections,
    ramps,
):
    rows, feat = queries.shape
    groups = lax.axis_size("fsdp")
    count = lax.axis_size("win")
    line = count // 2
    width = out_weight.shape[1]
    model = stream.shape[1]
    chans = head_weight.shape[1]
    cols = feat // groups
    heads = cols // HD
    window = lax.axis_index("win")
    member = lax.axis_index("fsdp")
    z = window // 2
    parity = window % 2
    regroup = width % LANES != 0 or line != 4
    blocks = line
    if regroup:
        blocks = max(b for b in (1, 2, 4) if (model // 2) % (b * LANES) == 0)
    span = model // 2 // blocks

    def group(value, bits):
        return lax.dynamic_slice(value, (0, (member ^ bits) * cols), (rows, cols))

    def pack(bits, *arrays):
        return jnp.stack([group(v, bits) for v in arrays])

    ids = jnp.stack([member, member ^ 2]).astype(jnp.int32)
    if regroup:
        sets = [[2 * a + p for a in range(line)] for p in range(2)]
        full = lax.all_gather(out_weight, "win", axis=1, tiled=True, axis_index_groups=sets)
        near = [[full[:, r * span : (r + 1) * span]] for r in range(blocks)]
        far = [[swap(b[0], "fsdp", 2)] for b in near]
        picks = [0] * blocks
        half_first = lambda v: jnp.swapaxes(v.reshape((line, 2, width) + v.shape[1:]), 0, 1)
        places = [(parity * blocks + r, r) for r in range(blocks)]
        ordered = half_first(stream.T).reshape(model, rows).T
        sent = [(1 - parity) * blocks + r for r in range(blocks)]
    else:
        down = [(a + 1, a) for a in range(line - 1)]
        up = [(a, a + 1) for a in range(line - 1)]
        on_down = [(a - 1, a - 2) for a in range(2, line)]
        on_up = [(a + 1, a + 2) for a in range(line - 2)]
        far_w = swap(out_weight, "fsdp", 2)
        near_up = line_move(out_weight, up)
        near_down = line_move(out_weight, down)
        half_first = lambda v: v
        ordered = stream
        sent = [2 * r + 1 - parity for r in range(blocks)]
    sizes = [(0, 0, heads), (1, 0, (heads + 1) // 2), (1, (heads + 1) // 2, heads // 2)]

    def packed(chunk):
        part, first, size = chunk
        at = slice(first * HD, (first + size) * HD)
        direct = pack(2 if part == 0 else 0, keys, values)[:, :, at]
        cross = pack(3 if part == 0 else 1, keys, values)[:, :, at]
        return direct, cross

    def sends(pair):
        return swap(pair[0], "fsdp", 2), swap(pair[1], "fsdp", 3)

    gate_b = half_first(gate).reshape(2 * blocks, 1, span)
    scale_b = half_first(head_scale).reshape(2 * blocks, 1, span)
    head_b = half_first(head_weight).reshape(2 * blocks, span, chans)
    shift_b = half_first(head_shift).reshape(2 * blocks, 1, span)
    vmem = pl.BlockSpec(memory_space=pltpu.VMEM)
    smem = pl.BlockSpec(memory_space=pltpu.SMEM)
    terms = pl.pallas_call(
        functools.partial(terms_kernel, blocks if regroup else 1),
        in_specs=[smem] + [vmem] * 3,
        out_specs=vmem,
        out_shape=jax.ShapeDtypeStruct((3, chans), jnp.float32),
        compiler_params=WHOLE,
    cost_estimate=pl.CostEstimate(
        flops=100 * model * chans, bytes_accessed=4 * model * chans, transcendentals=0
    ),
    )(parity.reshape(1).astype(jnp.int32), scale_b, shift_b, head_b)
    pair1, pair2 = packed(sizes[1]), packed(sizes[2])

    kv0 = sends(packed(sizes[0]))
    ring = [(i, (i + 1) % count) for i in range(count)]
    tail_latents = lax.ppermute(latents[latents.shape[0] - FD :], "win", ring)
    start_latents = lax.ppermute(latents[:FD], "win", [(j, i) for i, j in ring])
    mate = jnp.stack([pack(1, queries, keys, values), pack(3, queries, keys, values)])
    mate = swap(mate, "fsdp", 1)
    other_stream = jnp.stack(
        [lax.dynamic_slice(ordered, (0, b * span), (rows, span)) for b in sent]
    )
    other_stream = swap(other_stream, "win", 1)
    if not regroup:
        up2 = line_move(near_up, on_up)
        down2 = line_move(near_down, on_down)
        near2 = jnp.where(z >= 2, up2, down2)
        edge = line_move(near2, [(2, 3), (1, 0)])
        far_up = line_move(far_w, up)
        far_down = line_move(far_w, down)
    kv0, pair1 = after(kv0, pair1)
    kv1 = sends(pair1)

    def run(chunk, kv):
        return attend(ids, queries, keys, values, mate, *kv, *chunk, heads)

    att0 = run(sizes[0], kv0)
    att0_x = swap(att0, "win", 1)
    kv2 = sends(pair2)
    att1 = run(sizes[1], kv1)
    att1_x = swap(att1, "win", 1)
    if not regroup:
        ends = [
            ((w * groups + f), (w * groups + (f ^ 2)))
            for w in range(count)
            if w // 2 in (0, line - 1)
            for f in range(groups)
        ]
        far_edge = lax.ppermute(edge, ("win", "fsdp"), ends)
        far_up2 = line_move(far_up, on_up)
        far_down2 = line_move(far_down, on_down)
        at_top = (z == line - 1).astype(jnp.int32)
        at_end = ((z == line - 1) | (z == 0)).astype(jnp.int32)
        upper = (z >= 2).astype(jnp.int32)
        near = [[out_weight], [near_down, near_up], [near2], [near_up, edge]]
        far = [[far_w], [far_down, far_up], [far_down2, far_up2], [far_up, far_edge]]
        picks = [(0, 0), (at_top, at_top), (0, upper), (at_end, at_end)]
        steps = [0, jnp.where(z == line - 1, 3, 1), 2, jnp.where(z == line - 1, 1, 3)]
        places = [(2 * ((z + r) % line) + parity, (z + r) % line) for r in steps]
    else:
        picks = [(0, 0)] * blocks
    att2 = run(sizes[2], kv2)
    att2_x = swap(att2, "win", 1)

    frames = latents.shape[0]
    edge_rows = FD * rows // frames
    table = lambda entries: jnp.stack([jnp.asarray(e, jnp.int32) for e in entries])
    near_ids = table([p[0] for p in picks])
    far_ids = table([p[1] for p in picks])
    spots = table([p[0] for p in places] + [p[1] for p in places] + [parity])
    part = project(near_ids, (0, 1), (att0, att0_x), [[o] for o in near])
    rest = (att1, att2, att1_x, att2_x)
    far = [[o] for o in far]
    given = project(far_ids, (1,), rest, far, part)
    got = swap(given, "fsdp", 1)
    keep = project(far_ids, (0,), rest, far, part)
    sums = tally(spots, keep, got, ordered, other_stream, gate_b, scale_b, head_b, None, edge_rows)
    state = sums[0]
    _, across, ahead, behind, beside = sums
    got = swap(across, "win", 1)
    ahead = lax.ppermute(
        ahead,
        "win",
        [(2 * a + p, 2 * ((a + 1 - 2 * p) % line) + p) for a in range(line) for p in range(2)],
    )
    behind = lax.ppermute(
        behind,
        "win",
        [(2 * a + p, 2 * ((a - 1 + 2 * p) % line) + 1 - p) for a in range(line) for p in range(2)],
    )
    marks = jnp.stack([parity, window, (window + count - 1) % count]).astype(jnp.int32)
    return pl.pallas_call(
        functools.partial(finish_kernel, model),
        in_specs=[smem] * 4 + [vmem] * 9,
        out_specs=vmem,
        scratch_shapes=[
            pltpu.VMEM((rows, chans), jnp.float32),
            pltpu.VMEM((2, edge_rows, chans), jnp.float32),
        ],
        out_shape=jax.ShapeDtypeStruct(latents.shape, jnp.float32),
        compiler_params=WHOLE,
    )(
        marks, step_size, intersections, ramps.reshape(count, -1), state, beside, ahead,
        got, behind, terms, latents, tail_latents, start_latents
    )


def solution(mesh):
    in_specs = (
        P(("win", "fsdp"), None),
        P(("win", "fsdp"), None),
        P(("win", "fsdp"), None),
        P(("win", "fsdp"), None),
        P("fsdp", "win"),
        P(),
        P(),
        P(),
        P(),
        P("win", "fsdp"),
        P(),
        P(),
        P(),
    )
    out_specs = P("win", "fsdp")

    return jax.shard_map(local, mesh=mesh, in_specs=in_specs, out_specs=out_specs, check_vma=False)
```

time: 201 us -> 194 us (0.965)
  other arithmetic: 20 us -> 11.6 us
  local copies, waits for them, and re-layouts: 17.1 us -> 9.25 us
  waiting for transfers between devices: 70.5 us -> 77 us
  starting transfers between devices: 38.7 us -> 41 us
    ppermute x9, waiting for transfers between devices: 0.02 us -> 31.1 us  [line_move(): return lax.ppermute(value, 'win', pairs)]
    ppermute x15 -> x14, waiting for transfers between devices: 69.1 us -> 45.9 us  [swap(): return lax.ppermute(value, axis, [(i, i ^ bits) for i in range(size)])]
    unnamed x39 -> x13, local copies, waits for them, and re-layouts: 6.65 us -> 2.36 us
    mul x2 -> x0, other arithmetic: 2.4 us -> none  [the longest x1 1.33 us: local(): scaled = (head_scale[:, None] * head_f).reshape(line, 2, width, chans)]
    pallas_call x4 -> x6, Pallas kernels: 32.1 us -> 33.9 us  [the longest x3 22 us: project(): pl.pallas_call(functools.partial(project_kernel, halves, picks, len(att)...]
    ppermute x2 -> x4, starting transfers between devices: 5.14 us -> 6.88 us  [the longest x1 3.74 us: local(): start_latents = lax.ppermute(latents[:FD], 'win', [(j, i) for i, j in ring])]
    ppermute x15 -> x14, starting transfers between devices: 11.6 us -> 11.8 us  [swap(): return lax.ppermute(value, axis, [(i, i ^ bits) for i in range(size)])]
  transfers between devices with their start and end apart: 27 -> 28, of which waited for: 11 -> 9; matrix products, arithmetic and copies ran while one was open for 14% -> 10% of each run, Pallas kernels for 21% -> 19%
where the time goes in v2:
time: 194 us; the launch traced here: 193 us
  waiting for transfers between devices  77 us (40%)
  Pallas kernels  52.9 us (27%)
  starting transfers between devices  41 us (21%)
  other arithmetic  11.6 us (6%)
  local copies, waits for them, and re-layouts  9.25 us (5%)
    ppermute x14, waiting for transfers between devices, swap(): return lax.ppermute(value, axis, [(i, i ^ bits) for i in range(size)])  45.9 us
    ppermute x9, waiting for transfers between devices, line_move(): return lax.ppermute(value, 'win', pairs)  31.1 us
    pallas_call x3, Pallas kernels, project(): pl.pallas_call(functools.partial(project_kernel, halves, picks, len(att)...  22 us
    ppermute x9, starting transfers between devices, line_move(): return lax.ppermute(value, 'win', pairs)  19.2 us
    pallas_call x3, Pallas kernels, attend(): pl.pallas_call(functools.partial(attend_kernel, 1.0 / math.sqrt(HD)), gri...  19 us
    ppermute x14, starting transfers between devices, swap(): return lax.ppermute(value, axis, [(i, i ^ bits) for i in range(size)])  11.8 us
    pallas_call x1, Pallas kernels, tally(): pl.pallas_call(functools.partial(tally_kernel, state is None, edge > 0),...  6.01 us
    another operation x6, other arithmetic, pack(): return jnp.stack([group(v, bits) for v in arrays])  5.23 us
  transfers between devices with their start and end apart: 28, of which 9 were waited for; matrix products, arithmetic and copies ran while one was open for 10% of the time, Pallas kernels for 19%

profile of v2, /device:TPU:0, one launch (start us, length us, event | category | flops | bytes accessed | tf_op | source)
XLA Modules:
  0.0 192.8 jit_solution(5958173031597559867)
XLA Ops:
  0.0 5.9 %collective-permute-start.14 = (bf16[640,640]{1,0:T(8,128)(2,1)}, bf16[640,640]{1,0:T(8,128)(2,1)}, u32[]{:S(2)}, u32[]{:S(2)}) collective-permute-start(bf16[640,640]{1,0:T(8,128)(2,1)} %refs_2_.1), channel_id=1, source_target_pairs={{0,8},{4,12},{8,16},{12,20},{16,24},{20,28},{1,9},{5,13},{9,17},{1... | collective-permute-start | bytes 2457608 | tf_op jit(solution)/shard_map/ppermute | solution.py:28
  7.2 2.0 %dynamic-slice_bitcast_fusion.4 = (bf16[1,256,640]{2,1,0:T(8,128)(2,1)S(1)}, bf16[1,256,640]{2,1,0:T(8,128)(2,1)S(1)}, bf16[1,256,640]{2,1,0:T(8,128)(2,1)S(1)},...) fusion(bf16[256,2560]{1,0:T(8,128)(2,1)} %v_ref.5, ...), kind=kLoop, calls=%fused_computation.17 | loop fusion | bytes 5242896 | tf_op jit(solution)/shard_map/stack | solution.py:414
  10.8 1.5 collective-permute-start.9
  12.3 10.5 %collective-permute-done.14.refs_4_.refs_6_ = bf16[640,640]{1,0:T(8,128)(2,1)} collective-permute-done((bf16[640,640]{1,0:T(8,128)(2,1)}, bf16[640,640]{1,0:T(8,128)(2,1)}, u32[]{:S(2)}, u32[]{:S(2)}) %collective-permute-start.14) | collective-permute-done | bytes 819232 | tf_op jit(solution)/shard_map/ppermute | solution.py:28
  22.8 1.6 collective-permute-start.15
  24.3 3.5 %collective-permute-done.16.refs_3_ = bf16[640,640]{1,0:T(8,128)(2,1)} collective-permute-done((bf16[640,640]{1,0:T(8,128)(2,1)}, bf16[640,640]{1,0:T(8,128)(2,1)}, u32[]{:S(2)}, u32[]{:S(2)}) %collective-permute-start.16) | collective-permute-done | bytes 819232 | tf_op jit(solution)/shard_map/ppermute | solution.py:28
  30.0 1.5 collective-permute-start.1
  33.8 17.2 %collective-permute-done.17 = bf16[640,640]{1,0:T(8,128)(2,1)} collective-permute-done((bf16[640,640]{1,0:T(8,128)(2,1)}, bf16[640,640]{1,0:T(8,128)(2,1)}, u32[]{:S(2)}, u32[]{:S(2)}) %collective-permute-start.17) | collective-permute-done | bytes 819232 | tf_op jit(solution)/shard_map/ppermute | solution.py:28
  51.0 3.8 %collective-permute-start.11 = (bf16[640,640]{1,0:T(8,128)(2,1)}, bf16[640,640]{1,0:T(8,128)(2,1)}, u32[]{:S(2)}, u32[]{:S(2)}) collective-permute-start(bf16[640,640]{1,0:T(8,128)(2,1)} %collective-permute-done.9.refs_4_), channel_id=1, source_target_pairs={{0,8},{4,12},{8,16},{12,20},{16,24},{20,28},{1,9},{5,13},{9,17},{1... | collective-permute-start | bytes 2457608 | tf_op jit(solution)/shard_map/ppermute | solution.py:28
  54.8 2.1 %broadcast_select_fusion.refs_5_ = bf16[640,640]{1,0:T(8,128)(2,1)} fusion(bf16[640,640]{1,0:T(8,128)(2,1)} %collective-permute-done.15, bf16[640,640]{1,0:T(8,128)(2,1)} %collective-permute-done.17, pred[]{:T(512)S(6)} %ge.4), kind=kLoop, calls=%fused_computation.4 | loop fusion | flops 409600 | bytes 2457601 | tf_op jit(solution)/shard_map/jit(_where)/select_n | solution.py:481
  61.5 6.3 %collective-permute-done.5.far_ref = bf16[2,256,256]{2,1,0:T(8,128)(2,1)S(1)} collective-permute-done((bf16[2,256,256]{2,1,0:T(8,128)(2,1)S(1)}, bf16[2,256,256]{2,1,0:T(8,128)(2,1)S(1)}, u32[]{:S(2)}, u32[]{:S(2)}) %collective-permute-start.5) | collective-permute-done | bytes 262176 | tf_op jit(solution)/shard_map/ppermute | solution.py:23
  70.2 8.3 %shard_map.129.refs_0_ = bf16[2,256,640]{2,1,0:T(8,128)(2,1)} custom-call(s32[2]{0:T(128)} %pad_add_fusion.2.ids, bf16[256,2560]{1,0:T(8,128)(2,1)} %q_ref.5, bf16[256,2560]{1,0:T(8,128)(2,1)} %k_ref.5, bf16[256,2560]{1,0:T(8,128)(2,1)} %v_ref.5, bf16[2,3,256,640]{3,2,1,0:T(8,128)(2,1)} %collective-permute-done.mate_ref, ...), custom_call_target="tpu_custom_call" | custom-call | flops 1342177280 | bytes 3932160 | tf_op jit(solution)/shard_map/pallas_call | solution.py:57
  78.5 1.6 collective-permute-done.3.far_ref
  80.1 1.5 collective-permute-start.20
  82.9 1.6 collective-permute-start.13
  84.5 3.1 %collective-permute-start.19 = (bf16[640,640]{1,0:T(8,128)(2,1)}, bf16[640,640]{1,0:T(8,128)(2,1)}, u32[]{:S(2)}, u32[]{:S(2)}) collective-permute-start(bf16[640,640]{1,0:T(8,128)(2,1)} %collective-permute-done.18.refs_7_), channel_id=1, source_target_pairs={{0,2},{1,3},{2,0},{3,1},{4,6},{5,7},{6,4},{7,5},{24,26},{25,27},{2... | collective-permute-start | bytes 2457608 | tf_op jit(solution)/shard_map/ppermute | solution.py:503
  87.6 1.7 pad_maximum_fusion.4
  89.9 5.9 %shard_map.127.refs_0_ = bf16[2,256,384]{2,1,0:T(8,128)(2,1)} custom-call(s32[2]{0:T(128)} %pad_add_fusion.2.ids, bf16[256,2560]{1,0:T(8,128)(2,1)} %q_ref.5, bf16[256,2560]{1,0:T(8,128)(2,1)} %k_ref.5, bf16[256,2560]{1,0:T(8,128)(2,1)} %v_ref.5, bf16[2,3,256,640]{3,2,1,0:T(8,128)(2,1)} %collective-permute-done.mate_ref, ...), custom_call_target="tpu_custom_call" | custom-call | flops 805306368 | bytes 2359296 | tf_op jit(solution)/shard_map/pallas_call | solution.py:57
  95.9 14.2 %collective-permute-done.6.diag_ref = bf16[2,256,256]{2,1,0:T(8,128)(2,1)} collective-permute-done((bf16[2,256,256]{2,1,0:T(8,128)(2,1)}, bf16[2,256,256]{2,1,0:T(8,128)(2,1)}, u32[]{:S(2)}, u32[]{:S(2)}) %collective-permute-start.6) | collective-permute-done | bytes 262176 | tf_op jit(solution)/shard_map/ppermute | solution.py:23
  111.9 4.8 %shard_map.128.refs_1_ = bf16[2,256,256]{2,1,0:T(8,128)(2,1)} custom-call(s32[2]{0:T(128)} %pad_add_fusion.2.ids, bf16[256,2560]{1,0:T(8,128)(2,1)} %q_ref.5, bf16[256,2560]{1,0:T(8,128)(2,1)} %k_ref.5, bf16[256,2560]{1,0:T(8,128)(2,1)} %v_ref.5, bf16[2,3,256,640]{3,2,1,0:T(8,128)(2,1)} %collective-permute-done.mate_ref, bf16[2,256,256]{2,1,0:T(8,128)(2,1)} %copy-done.4, ...), custom_call_target="tpu_custom_call" | custom-call | flops 536870912 | bytes 1572864 | tf_op jit(solution)/shard_map/pallas_call | solution.py:57
  117.6 8.5 %shard_map.130.refs_11_ = bf16[4,2,2,256,640]{4,3,2,1,0:T(8,128)(2,1)} custom-call(s32[4]{0:T(128)} %add_add_fusion.1.ids, bf16[2,256,640]{2,1,0:T(8,128)(2,1)} %shard_map.129.refs_0_, bf16[2,256,640]{2,1,0:T(8,128)(2,1)} %collective-permute-done.20.refs_1_, bf16[640,640]{1,0:T(8,128)(2,1)} %refs_2_.1, bf16[640,640]{1,0:T(8,128)(2,1)} %collective-permute-done.16.refs_3_, ...), custom_call_target="tpu_custom_call" | custom-call | flops 3355443200 | bytes 4587520 | tf_op jit(solution)/shard_map/pallas_call | solution.py:160
  126.1 1.8 collective-permute-done.8.refs_3_
  127.9 6.7 %shard_map.132 = bf16[4,1,2,256,640]{4,3,2,1,0:T(8,128)(2,1)} custom-call(s32[4]{0:T(128)} %add_add_fusion.ids, bf16[2,256,384]{2,1,0:T(8,128)(2,1)} %shard_map.127.refs_0_, bf16[2,256,256]{2,1,0:T(8,128)(2,1)} %shard_map.128.refs_1_, bf16[2,256,384]{2,1,0:T(8,128)(2,1)} %collective-permute-done.7.refs_2_, ...), custom_call_target="tpu_custom_call" | custom-call | flops 1677721600 | bytes 4587520 | tf_op jit(solution)/shard_map/pallas_call | solution.py:160
  134.7 1.4 dynamic-slice_bitcast_fusion.3
  138.5 1.4 copy.14
  140.6 6.7 %shard_map.131.keep_ref = bf16[4,1,2,256,640]{4,3,2,1,0:T(8,128)(2,1)} custom-call(s32[4]{0:T(128)} %add_add_fusion.ids, bf16[2,256,384]{2,1,0:T(8,128)(2,1)} %shard_map.127.refs_0_, bf16[2,256,256]{2,1,0:T(8,128)(2,1)} %shard_map.128.refs_1_, bf16[2,256,384]{2,1,0:T(8,128)(2,1)} %collective-permute-done.7.refs_2_, ...), custom_call_target="tpu_custom_call" | custom-call | flops 1677721600 | bytes 4587520 | tf_op jit(solution)/shard_map/pallas_call | solution.py:160
  147.4 21.5 %collective-permute-done.22.other_ref = bf16[4,256,640]{2,1,0:T(8,128)(2,1)} collective-permute-done((bf16[4,256,640]{2,1,0:T(8,128)(2,1)}, bf16[4,256,640]{2,1,0:T(8,128)(2,1)}, u32[]{:S(2)}, u32[]{:S(2)}) %collective-permute-start.22) | collective-permute-done | bytes 1310752 | tf_op jit(solution)/shard_map/ppermute | solution.py:23
  168.9 6.0 %shard_map.133 = (f32[2,256,128]{2,1,0:T(8,128)}, f32[320,128]{1,0:T(8,128)}, f32[64,128]{1,0:T(8,128)}, f32[64,128]{1,0:T(8,128)}, f32[64,128]{1,0:T(8,128)}) custom-call(s32[9]{0:T(128)} %stack.169.ids, bf16[4,1,2,256,640]{4,3,2,1,0:T(8,128)(2,1)} %shard_map.131.keep_ref, bf16[4,1,2,256,640]{4,3,2,1,0:T(8,128)(2,1)} %collective-permute-done.21.got_ref, ...), custom_call_target="tpu_custom_call" | custom-call | flops 188743680 | bytes 7864320 | tf_op jit(solution)/shard_map/pallas_call | solution.py:260
  178.4 3.7 %collective-permute-start.27 = (f32[4,1024]{1,0:T(4,128)}, f32[4,1024]{1,0:T(4,128)}, u32[]{:S(2)}, u32[]{:S(2)}) collective-permute-start(f32[4,1024]{1,0:T(4,128)} %get-tuple-element.37), channel_id=1, source_target_pairs={{4,0},{8,4},{12,8},{16,12},{20,16},{24,20},{28,24},{0,28},{5,1},{9... | collective-permute-start | bytes 49160 | tf_op jit(solution)/shard_map/ppermute | solution.py:471
  182.1 2.2 %collective-permute-start.25 = (f32[64,128]{1,0:T(8,128)}, f32[64,128]{1,0:T(8,128)}, u32[]{:S(2)}, u32[]{:S(2)}) collective-permute-start(f32[64,128]{1,0:T(8,128)} %get-tuple-element.22), channel_id=1, source_target_pairs={{0,28},{4,8},{8,4},{12,16},{16,12},{20,24},{24,20},{28,0},{1,29},{... | collective-permute-start | bytes 98312 | tf_op jit(solution)/shard_map/ppermute | solution.py:540
  186.9 3.3 %shard_map.134.terms_ref = f32[3,64]{1,0:T(4,128)} custom-call(s32[1]{0:T(128)} %bitcast.odd_ref, f32[8,1,640]{2,1,0:T(1,128)} %bitcast.56, f32[8,1,640]{2,1,0:T(1,128)} %bitcast.58, bf16[8,640,64]{2,1,0:T(8,128)(2,1)} %bitcast.54), custom_call_target="tpu_custom_call" | custom-call | flops 32768000 | bytes 1310720 | tf_op jit(solution)/shard_map/pallas_call | solution.py:456
  190.2 2.6 %shard_map.135 = f32[16,1024]{1,0:T(8,128)} custom-call(s32[3]{0:T(128)} %pad_add_fusion.ids, f32[1]{0:T(128)S(6)} %copy.16.step_ref, s32[8]{0:T(128)} %shares_ref.1, s32[8,8]{1,0:T(8,128)} %copy.15.ramps_ref, f32[2,256,128]{2,1,0:T(8,128)} %get-tuple-element.18.mine_ref, f32[64,128]{1,0:T(8,128)} %get-tuple-element.19.beside_ref, ...), custom_call_target="tpu_custom_call" | custom-call | tf_op jit(solution)/shard_map/pallas_call | solution.py:546
  (67 shorter events, 27.5 us)
Async XLA Ops:
  0.0 22.8 %collective-permute-start.14 = (bf16[640,640]{1,0:T(8,128)(2,1)}, bf16[640,640]{1,0:T(8,128)(2,1)}, u32[]{:S(2)}, u32[]{:S(2)}) collective-permute-start(bf16[640,640]{1,0:T(8,128)(2,1)} %refs_2_.1), channel_id=1, source_target_pairs={{0,8},{4,12},{8,16},{12,20},{16,24},{20,28},{1,9},{5,13},{9,17},{1... | collective-permute-start | bytes 2457608 | tf_op jit(solution)/shard_map/ppermute | solution.py:28
  5.9 21.9 %collective-permute-start.16 = (bf16[640,640]{1,0:T(8,128)(2,1)}, bf16[640,640]{1,0:T(8,128)(2,1)}, u32[]{:S(2)}, u32[]{:S(2)}) collective-permute-start(bf16[640,640]{1,0:T(8,128)(2,1)} %refs_2_.1), channel_id=1, source_target_pairs={{8,0},{12,4},{16,8},{20,12},{24,16},{28,20},{9,1},{13,5},{17,9},{2... | collective-permute-start | bytes 2457608 | tf_op jit(solution)/shard_map/ppermute | solution.py:28
  7.2 2.1 %copy-start = (bf16[256,2560]{1,0:T(8,128)(2,1)S(1)}, bf16[256,2560]{1,0:T(8,128)(2,1)}, u32[]{:S(2)}) copy-start(bf16[256,2560]{1,0:T(8,128)(2,1)} %q_ref.5) | copy-start | bytes 3932164
  9.3 51.4 %copy-start.1 = (bf16[1,256,640]{2,1,0:T(8,128)(2,1)}, bf16[1,256,640]{2,1,0:T(8,128)(2,1)S(1)}, u32[]{:S(2)}) copy-start(bf16[1,256,640]{2,1,0:T(8,128)(2,1)S(1)} %get-tuple-element.30) | copy-start | bytes 983044
  9.3 51.4 %copy-start.2 = (bf16[1,256,640]{2,1,0:T(8,128)(2,1)}, bf16[1,256,640]{2,1,0:T(8,128)(2,1)S(1)}, u32[]{:S(2)}) copy-start(bf16[1,256,640]{2,1,0:T(8,128)(2,1)S(1)} %get-tuple-element.39) | copy-start | bytes 983044
  9.9 58.7 %collective-permute-start = (bf16[2,3,256,640]{3,2,1,0:T(8,128)(2,1)S(1)}, bf16[2,3,256,640]{3,2,1,0:T(8,128)(2,1)}, u32[]{:S(2)}, u32[]{:S(2)}) collective-permute-start(bf16[2,3,256,640]{3,2,1,0:T(8,128)(2,1)S(1)} %pad_maximum_fusion), channel_id=1, source_target_pairs={{0,1},{1,0},{2,3},{3,2},{4,5},{5,4},{6,7},{7,6},{8,9},{9,8},{10,11... | collective-permute-start | bytes 5898248 | tf_op jit(solution)/shard_map/ppermute | solution.py:23
  10.8 21.7 %collective-permute-start.9 = (bf16[640,640]{1,0:T(8,128)(2,1)S(1)}, bf16[640,640]{1,0:T(8,128)(2,1)}, u32[]{:S(2)}, u32[]{:S(2)}) collective-permute-start(bf16[640,640]{1,0:T(8,128)(2,1)S(1)} %copy-done.5), channel_id=1, source_target_pairs={{0,2},{1,3},{2,0},{3,1},{4,6},{5,7},{6,4},{7,5},{8,10},{9,11},{10,... | collective-permute-start | bytes 2457608 | tf_op jit(solution)/shard_map/ppermute | solution.py:23
  22.8 9.7 %collective-permute-start.15 = (bf16[640,640]{1,0:T(8,128)(2,1)}, bf16[640,640]{1,0:T(8,128)(2,1)}, u32[]{:S(2)}, u32[]{:S(2)}) collective-permute-start(bf16[640,640]{1,0:T(8,128)(2,1)} %collective-permute-done.14.refs_4_.refs_6_), channel_id=1, source_target_pairs={{8,16},{12,20},{16,24},{20,28},{9,17},{13,21},{17,25},{21,29},{10,... | collective-permute-start | bytes 2457608 | tf_op jit(solution)/shard_map/ppermute | solution.py:28
  27.8 23.3 %collective-permute-start.17 = (bf16[640,640]{1,0:T(8,128)(2,1)}, bf16[640,640]{1,0:T(8,128)(2,1)}, u32[]{:S(2)}, u32[]{:S(2)}) collective-permute-start(bf16[640,640]{1,0:T(8,128)(2,1)} %collective-permute-done.16.refs_3_), channel_id=1, source_target_pairs={{8,0},{12,4},{16,8},{20,12},{9,1},{13,5},{17,9},{21,13},{10,2},{14... | collective-permute-start | bytes 2457608 | tf_op jit(solution)/shard_map/ppermute | solution.py:28
  30.0 26.9 %collective-permute-start.1 = (bf16[2,256,640]{2,1,0:T(8,128)(2,1)}, bf16[2,256,640]{2,1,0:T(8,128)(2,1)}, u32[]{:S(2)}, u32[]{:S(2)}) collective-permute-start(bf16[2,256,640]{2,1,0:T(8,128)(2,1)} %pad_maximum_fusion.2), channel_id=1, source_target_pairs={{0,2},{1,3},{2,0},{3,1},{4,6},{5,7},{6,4},{7,5},{8,10},{9,11},{10,... | collective-permute-start | bytes 1966088 | tf_op jit(solution)/shard_map/ppermute | solution.py:23
  32.5 26.3 %collective-permute-start.2 = (bf16[2,256,640]{2,1,0:T(8,128)(2,1)}, bf16[2,256,640]{2,1,0:T(8,128)(2,1)}, u32[]{:S(2)}, u32[]{:S(2)}) collective-permute-start(bf16[2,256,640]{2,1,0:T(8,128)(2,1)} %pad_maximum_fusion.3), channel_id=1, source_target_pairs={{0,3},{1,2},{2,1},{3,0},{4,7},{5,6},{6,5},{7,4},{8,11},{9,10},{10,... | collective-permute-start | bytes 1966088 | tf_op jit(solution)/shard_map/ppermute | solution.py:23
  32.5 49.1 %collective-permute-start.10 = (bf16[640,640]{1,0:T(8,128)(2,1)}, bf16[640,640]{1,0:T(8,128)(2,1)}, u32[]{:S(2)}, u32[]{:S(2)}) collective-permute-start(bf16[640,640]{1,0:T(8,128)(2,1)} %collective-permute-done.9.refs_4_), channel_id=1, source_target_pairs={{8,0},{12,4},{16,8},{20,12},{24,16},{28,20},{9,1},{13,5},{17,9},{2... | collective-permute-start | bytes 2457608 | tf_op jit(solution)/shard_map/ppermute | solution.py:28
  51.0 31.9 %collective-permute-start.11 = (bf16[640,640]{1,0:T(8,128)(2,1)}, bf16[640,640]{1,0:T(8,128)(2,1)}, u32[]{:S(2)}, u32[]{:S(2)}) collective-permute-start(bf16[640,640]{1,0:T(8,128)(2,1)} %collective-permute-done.9.refs_4_), channel_id=1, source_target_pairs={{0,8},{4,12},{8,16},{12,20},{16,24},{20,28},{1,9},{5,13},{9,17},{1... | collective-permute-start | bytes 2457608 | tf_op jit(solution)/shard_map/ppermute | solution.py:28
  57.0 27.5 %collective-permute-start.18 = (bf16[640,640]{1,0:T(8,128)(2,1)}, bf16[640,640]{1,0:T(8,128)(2,1)}, u32[]{:S(2)}, u32[]{:S(2)}) collective-permute-start(bf16[640,640]{1,0:T(8,128)(2,1)} %broadcast_select_fusion.refs_5_), channel_id=1, source_target_pairs={{16,24},{20,28},{8,0},{12,4},{17,25},{21,29},{9,1},{13,5},{18,26},... | collective-permute-start | bytes 2457608 | tf_op jit(solution)/shard_map/ppermute | solution.py:28
  58.8 9.1 %collective-permute-start.5 = (bf16[2,256,256]{2,1,0:T(8,128)(2,1)S(1)}, bf16[2,256,256]{2,1,0:T(8,128)(2,1)S(1)}, u32[]{:S(2)}, u32[]{:S(2)}) collective-permute-start(bf16[2,256,256]{2,1,0:T(8,128)(2,1)S(1)} %pad_maximum_fusion.5), channel_id=1, source_target_pairs={{0,2},{1,3},{2,0},{3,1},{4,6},{5,7},{6,4},{7,5},{8,10},{9,11},{10,... | collective-permute-start | bytes 786440 | tf_op jit(solution)/shard_map/ppermute | solution.py:23
  67.8 12.3 %collective-permute-start.3 = (bf16[2,256,384]{2,1,0:T(8,128)(2,1)}, bf16[2,256,384]{2,1,0:T(8,128)(2,1)}, u32[]{:S(2)}, u32[]{:S(2)}) collective-permute-start(bf16[2,256,384]{2,1,0:T(8,128)(2,1)} %fusion.1), channel_id=1, source_target_pairs={{0,2},{1,3},{2,0},{3,1},{4,6},{5,7},{6,4},{7,5},{8,10},{9,11},{10,... | collective-permute-start | bytes 1179656 | tf_op jit(solution)/shard_map/ppermute | solution.py:23
  68.5 20.8 %collective-permute-start.4 = (bf16[2,256,384]{2,1,0:T(8,128)(2,1)}, bf16[2,256,384]{2,1,0:T(8,128)(2,1)}, u32[]{:S(2)}, u32[]{:S(2)}) collective-permute-start(bf16[2,256,384]{2,1,0:T(8,128)(2,1)} %fusion), channel_id=1, source_target_pairs={{0,3},{1,2},{2,1},{3,0},{4,7},{5,6},{6,5},{7,4},{8,11},{9,10},{10,... | collective-permute-start | bytes 1179656 | tf_op jit(solution)/shard_map/ppermute | solution.py:23
  80.1 36.5 %collective-permute-start.20 = (bf16[2,256,640]{2,1,0:T(8,128)(2,1)}, bf16[2,256,640]{2,1,0:T(8,128)(2,1)}, u32[]{:S(2)}, u32[]{:S(2)}) collective-permute-start(bf16[2,256,640]{2,1,0:T(8,128)(2,1)} %shard_map.129.refs_0_), channel_id=1, source_target_pairs={{0,4},{4,0},{8,12},{12,8},{16,20},{20,16},{24,28},{28,24},{1,5},{5... | collective-permute-start | bytes 1966088 | tf_op jit(solution)/shard_map/ppermute | solution.py:23
  81.6 46.2 %collective-permute-start.12 = (bf16[640,640]{1,0:T(8,128)(2,1)}, bf16[640,640]{1,0:T(8,128)(2,1)}, u32[]{:S(2)}, u32[]{:S(2)}) collective-permute-start(bf16[640,640]{1,0:T(8,128)(2,1)} %collective-permute-done.10.refs_5_), channel_id=1, source_target_pairs={{8,0},{12,4},{16,8},{20,12},{9,1},{13,5},{17,9},{21,13},{10,2},{14... | collective-permute-start | bytes 2457608 | tf_op jit(solution)/shard_map/ppermute | solution.py:28
  82.9 45.0 %collective-permute-start.13 = (bf16[640,640]{1,0:T(8,128)(2,1)}, bf16[640,640]{1,0:T(8,128)(2,1)}, u32[]{:S(2)}, u32[]{:S(2)}) collective-permute-start(bf16[640,640]{1,0:T(8,128)(2,1)} %collective-permute-done.11.refs_6_.refs_9_), channel_id=1, source_target_pairs={{8,16},{12,20},{16,24},{20,28},{9,17},{13,21},{17,25},{21,29},{10,... | collective-permute-start | bytes 2457608 | tf_op jit(solution)/shard_map/ppermute | solution.py:28
  84.5 43.4 %collective-permute-start.19 = (bf16[640,640]{1,0:T(8,128)(2,1)}, bf16[640,640]{1,0:T(8,128)(2,1)}, u32[]{:S(2)}, u32[]{:S(2)}) collective-permute-start(bf16[640,640]{1,0:T(8,128)(2,1)} %collective-permute-done.18.refs_7_), channel_id=1, source_target_pairs={{0,2},{1,3},{2,0},{3,1},{4,6},{5,7},{6,4},{7,5},{24,26},{25,27},{2... | collective-permute-start | bytes 2457608 | tf_op jit(solution)/shard_map/ppermute | solution.py:503
  89.3 20.7 %collective-permute-start.6 = (bf16[2,256,256]{2,1,0:T(8,128)(2,1)}, bf16[2,256,256]{2,1,0:T(8,128)(2,1)}, u32[]{:S(2)}, u32[]{:S(2)}) collective-permute-start(bf16[2,256,256]{2,1,0:T(8,128)(2,1)} %pad_maximum_fusion.4), channel_id=1, source_target_pairs={{0,3},{1,2},{2,1},{3,0},{4,7},{5,6},{6,5},{7,4},{8,11},{9,10},{10,... | collective-permute-start | bytes 786440 | tf_op jit(solution)/shard_map/ppermute | solution.py:23
  110.1 17.8 %collective-permute-start.7 = (bf16[2,256,384]{2,1,0:T(8,128)(2,1)}, bf16[2,256,384]{2,1,0:T(8,128)(2,1)}, u32[]{:S(2)}, u32[]{:S(2)}) collective-permute-start(bf16[2,256,384]{2,1,0:T(8,128)(2,1)} %shard_map.127.refs_0_), channel_id=1, source_target_pairs={{0,4},{4,0},{8,12},{12,8},{16,20},{20,16},{24,28},{28,24},{1,5},{5... | collective-permute-start | bytes 1179656 | tf_op jit(solution)/shard_map/ppermute | solution.py:23
  116.7 11.2 %collective-permute-start.8 = (bf16[2,256,256]{2,1,0:T(8,128)(2,1)}, bf16[2,256,256]{2,1,0:T(8,128)(2,1)}, u32[]{:S(2)}, u32[]{:S(2)}) collective-permute-start(bf16[2,256,256]{2,1,0:T(8,128)(2,1)} %shard_map.128.refs_1_), channel_id=1, source_target_pairs={{0,4},{4,0},{8,12},{12,8},{16,20},{20,16},{24,28},{28,24},{1,5},{5... | collective-permute-start | bytes 786440 | tf_op jit(solution)/shard_map/ppermute | solution.py:23
  134.6 34.3 %collective-permute-start.21 = (bf16[4,1,2,256,640]{4,3,2,1,0:T(8,128)(2,1)}, bf16[4,1,2,256,640]{4,3,2,1,0:T(8,128)(2,1)}, u32[]{:S(2)}, u32[]{:S(2)}) collective-permute-start(bf16[4,1,2,256,640]{4,3,2,1,0:T(8,128)(2,1)} %shard_map.132), channel_id=1, source_target_pairs={{0,1},{1,0},{2,3},{3,2},{4,5},{5,4},{6,7},{7,6},{8,9},{9,8},{10,11... | collective-permute-start | bytes 7864328 | tf_op jit(solution)/shard_map/ppermute | solution.py:23
  136.1 2.4 %copy-start.3 = (bf16[5120,64]{0,1:T(8,128)(2,1)S(1)}, bf16[5120,64]{0,1:T(8,128)(2,1)}, u32[]{:S(2)}) copy-start(bf16[5120,64]{0,1:T(8,128)(2,1)} %param.21) | copy-start | bytes 1966084
  137.4 31.5 %collective-permute-start.22 = (bf16[4,256,640]{2,1,0:T(8,128)(2,1)}, bf16[4,256,640]{2,1,0:T(8,128)(2,1)}, u32[]{:S(2)}, u32[]{:S(2)}) collective-permute-start(bf16[4,256,640]{2,1,0:T(8,128)(2,1)} %pad_maximum_fusion.1), channel_id=1, source_target_pairs={{0,4},{4,0},{8,12},{12,8},{16,20},{20,16},{24,28},{28,24},{1,5},{5... | collective-permute-start | bytes 3932168 | tf_op jit(solution)/shard_map/ppermute | solution.py:23
  174.9 15.3 %collective-permute-start.24 = (f32[320,128]{1,0:T(8,128)}, f32[320,128]{1,0:T(8,128)}, u32[]{:S(2)}, u32[]{:S(2)}) collective-permute-start(f32[320,128]{1,0:T(8,128)} %get-tuple-element.21), channel_id=1, source_target_pairs={{0,4},{4,0},{8,12},{12,8},{16,20},{20,16},{24,28},{28,24},{1,5},{5... | collective-permute-start | bytes 491528 | tf_op jit(solution)/shard_map/ppermute | solution.py:23
  177.4 12.8 %collective-permute-start.26 = (f32[4,1024]{1,0:T(4,128)}, f32[4,1024]{1,0:T(4,128)}, u32[]{:S(2)}, u32[]{:S(2)}) collective-permute-start(f32[4,1024]{1,0:T(4,128)} %get-tuple-element.38), channel_id=1, source_target_pairs={{0,4},{4,8},{8,12},{12,16},{16,20},{20,24},{24,28},{28,0},{1,5},{5... | collective-permute-start | bytes 49160 | tf_op jit(solution)/shard_map/ppermute | solution.py:470
  178.4 11.8 %collective-permute-start.27 = (f32[4,1024]{1,0:T(4,128)}, f32[4,1024]{1,0:T(4,128)}, u32[]{:S(2)}, u32[]{:S(2)}) collective-permute-start(f32[4,1024]{1,0:T(4,128)} %get-tuple-element.37), channel_id=1, source_target_pairs={{4,0},{8,4},{12,8},{16,12},{20,16},{24,20},{28,24},{0,28},{5,1},{9... | collective-permute-start | bytes 49160 | tf_op jit(solution)/shard_map/ppermute | solution.py:471
  182.1 8.1 %collective-permute-start.23 = (f32[64,128]{1,0:T(8,128)}, f32[64,128]{1,0:T(8,128)}, u32[]{:S(2)}, u32[]{:S(2)}) collective-permute-start(f32[64,128]{1,0:T(8,128)} %get-tuple-element.20), channel_id=1, source_target_pairs={{0,8},{4,28},{8,16},{12,4},{16,24},{20,12},{24,0},{28,20},{1,9},{5... | collective-permute-start | bytes 98312 | tf_op jit(solution)/shard_map/ppermute | solution.py:535
  182.1 8.1 %collective-permute-start.25 = (f32[64,128]{1,0:T(8,128)}, f32[64,128]{1,0:T(8,128)}, u32[]{:S(2)}, u32[]{:S(2)}) collective-permute-start(f32[64,128]{1,0:T(8,128)} %get-tuple-element.22), channel_id=1, source_target_pairs={{0,28},{4,8},{8,4},{12,16},{16,12},{20,24},{24,20},{28,0},{1,29},{... | collective-permute-start | bytes 98312 | tf_op jit(solution)/shard_map/ppermute | solution.py:540
  (2 other events, 1.9 us)
